TPU v7x, 32 devices: a whole 2x2x4 slice. The times are simulated.
32 devices in a mesh: graph: 8 (over y, x, core), rep: 4 (over z).
Axes of the slice: x: 2, y: 2, z: 4, core: 2. Of those that a mesh axis runs over, the one named last changes fastest.
Arguments:
- nodes: bfloat16 [4, 64, 32, 256], P('rep', 'graph'), may hold values from -20 to 20, as said below
- cotangent: bfloat16 [4, 64, 32, 256], P('rep', 'graph'), may hold values from -6 to 6
- live: int32 [4, 64], P('rep', 'graph'), may hold values from 2 to 32, as said below
- partner_first: int32 [4, 64], P('rep', 'graph'), may hold values from 0 to 63, as said below
- partner_size: int32 [4, 64], P('rep', 'graph'), may hold values from 1 to 2
- edge_src: int32 [4, 2048], P('rep', 'graph'), may hold values from 0 to 255, as said below
- edge_dst: int32 [4, 2048], P('rep', 'graph'), may hold values from 0 to 255, as said below
- w_edge1: bfloat16 [512, 512], replicated, may hold values from -0.25 to 0.25
- b_edge: float32 [512], replicated, may hold values from -3 to 3
- w_edge2: bfloat16 [512, 256], replicated, may hold values from -0.25 to 0.25
- w_node1: bfloat16 [768, 512], replicated, may hold values from -0.21875 to 0.21875
- b_node: float32 [512], replicated, may hold values from -3 to 3
- w_node2: bfloat16 [512, 256], replicated, may hold values from -0.25 to 0.25
Outputs:
- updated: bfloat16 [4, 64, 32, 256], P('rep', 'graph')
- d_nodes: bfloat16 [4, 64, 32, 256], P('rep', 'graph')
- g_edge1: float32 [512, 512], P('rep')
- g_bedge: float32 [512], P('rep')
- g_edge2: float32 [512, 256], P('rep')
- g_node1: float32 [768, 512], P('rep')
- g_bnode: float32 [512], P('rep')
- g_node2: float32 [512, 256], P('rep')
Inputs may be any that keep to these rules, and one draw needn't show every extreme that they name: A graph is one or two consecutive granules of one device, and every granule of a graph but its last is full; rows beyond live are padding. `partner_first`: index within the replica of the first granule of the partner graph, the same for all granules of a graph; pairing is mutual. Graphs in the lower half of a device's 8 granules pair with graphs in the upper half of some device's granules; the upper-half graphs of one device have partners on distinct devices. Within a replica every half of every device holds the same number of two-granule graphs. `edge_src`: row index within the device (granule times 32 plus row); both ends of an edge are live rows of the same graph. `edge_dst`: as edge_src. `nodes`: padding rows are zero.
All inputs are finite; a program needn't handle non-finite values.
Results may differ from a plain program's by a relative error of at most 0.023.
Values may be sent and summed in bfloat16 or wider, within the bound.
A program may use at most 128 MiB of HBM per device.

v0:
```python
import functools

import jax
import jax.numpy as jnp
from jax import lax
from jax.experimental import pallas as pl
from jax.experimental.pallas import tpu as pltpu
from jax.sharding import PartitionSpec as P

GMAX = 2
LANES = 128
F32 = jnp.float32
BF16 = jnp.bfloat16


def dot_nn(a, b):
    return lax.dot_general(a, b, (((1,), (0,)), ((), ())), preferred_element_type=F32)


def dot_nt(a, b):
    return lax.dot_general(a, b, (((1,), (1,)), ((), ())), preferred_element_type=F32)


def dot_tn(a, b):
    return lax.dot_general(a, b, (((0,), (0,)), ((), ())), preferred_element_type=F32)


def sigmoid(v):
    return 1.0 / (1.0 + jnp.exp(-v))


def silu_slope(v, s):
    return s * (1.0 + v * (1.0 - s))


def round_up(value, unit):
    return -(-value // unit) * unit


def send(src, dst, send_sem, recv_sem, graph, rep):
    return pltpu.make_async_remote_copy(
        src_ref=src,
        dst_ref=dst,
        send_sem=send_sem,
        recv_sem=recv_sem,
        device_id={"graph": graph, "rep": rep},
        device_id_type=pl.DeviceIdType.MESH,
    )


class Reduce:
    def __init__(self, n_graph, n_rep, me, rep, refs):
        self.n, self.r, self.me, self.rep = n_graph, n_rep, me, rep
        (self.full, self.r0, self.a, self.r1, self.b, self.r2, self.got,
         self.s0, self.s1, self.v1, self.s2, self.v2, self.s3, self.v3) = refs
        self.chips = n_graph // 2
        self.core = lax.rem(me, 2)
        self.chip = lax.div(me, 2)
        self.half = self.full.shape[1] // 2
        self.ch = self.full.shape[1] // n_graph
        self.sends = []

    def go(self, copy):
        copy.start()
        self.sends.append(copy)

    def rows(self, start, size):
        return pl.ds(pl.multiple_of(start, 16), size)

    def start_core(self):
        other = 1 - self.core
        self.c0 = send(self.full.at[:, self.rows(other * self.half, self.half), :], self.r0,
                       self.s0.at[0], self.s0.at[1], self.chip * 2 + other, self.rep)
        self.go(self.c0)

    def start_plane(self):
        self.c0.wait_recv()
        mine = self.full[:, self.rows(self.core * self.half, self.half), :].astype(F32)
        self.a[...] = (mine + self.r0[...].astype(F32)).astype(BF16)
        self.c1 = []
        for d in range(1, self.chips):
            q = lax.rem(self.chip + d, self.chips)
            copy = send(self.a.at[:, self.rows(q * self.ch, self.ch), :], self.r1.at[d],
                        self.s1.at[d], self.v1.at[d], q * 2 + self.core, self.rep)
            self.go(copy)
            self.c1.append(copy)

    def start_rep(self):
        total = self.a[:, self.rows(self.chip * self.ch, self.ch), :].astype(F32)
        for copy in self.c1:
            copy.wait_recv()
        for d in range(1, self.chips):
            total = total + self.r1[d].astype(F32)
        self.b[...] = total.astype(BF16)
        self.c2 = []
        for d in range(1, self.r):
            z = lax.rem(self.rep + d, self.r)
            copy = send(self.b.at[z], self.r2.at[d], self.s2.at[d], self.v2.at[d], self.me, z)
            self.go(copy)
            self.c2.append(copy)

    def start_gather(self):
        total = self.b[self.rep].astype(F32)
        for copy in self.c2:
            copy.wait_recv()
        for d in range(1, self.r):
            total = total + self.r2[d].astype(F32)
        place = self.core * self.chips + self.chip
        self.got[place] = total.astype(BF16)
        self.c3 = []
        for d in range(1, self.chips):
            to = lax.rem(self.chip + d, self.chips)
            src = self.core * self.chips + lax.rem(self.chip + self.chips - d, self.chips)
            self.go(send(self.got.at[place], self.got.at[place], self.s3.at[d], self.v3.at[d],
                         to * 2 + self.core, self.rep))
            self.c3.append(send(self.got.at[src], self.got.at[src], self.s3.at[d], self.v3.at[d],
                                to * 2 + self.core, self.rep))

    def start_swap(self):
        for copy in self.c3:
            copy.wait_recv()
        other = 1 - self.core
        mine = self.got.at[pl.ds(self.core * self.chips, self.chips)]
        theirs = self.got.at[pl.ds(other * self.chips, self.chips)]
        to = self.chip * 2 + other
        self.go(send(mine, mine, self.s3.at[0], self.v3.at[0], to, self.rep))
        self.c4 = send(theirs, theirs, self.s3.at[0], self.v3.at[0], to, self.rep)

    def finish(self, out):
        self.c4.wait_recv()
        out[...] = self.got[...].reshape(self.n * self.ch, LANES)

    def drain(self):
        for copy in self.sends:
            copy.wait_send()


def put_grad(full, offset, grad, n_rep):
    share = grad.shape[0] // n_rep
    panels = grad.shape[1] // LANES
    low = grad.astype(BF16)
    for j in range(panels):
        full[:, offset + j * share : offset + (j + 1) * share, :] = low[
            :, j * LANES : (j + 1) * LANES
        ].reshape(n_rep, share, LANES)
    return offset + panels * share


def put_bias(full, offset, bias, n_rep):
    share = bias.shape[1] // n_rep
    count = full.shape[1] - offset
    first = lax.broadcasted_iota(jnp.int32, (count, LANES), 0) == 0
    for r in range(n_rep):
        row = bias[:, r * share : (r + 1) * share]
        if share < LANES:
            row = jnp.concatenate([row, jnp.zeros((1, LANES - share), F32)], axis=1)
        full[r, offset:, :] = jnp.where(first, row, 0.0).astype(BF16)


def take_grad(flat, offset, out, scale):
    share = out.shape[0]
    panels = out.shape[1] // LANES
    for j in range(panels):
        out[:, j * LANES : (j + 1) * LANES] = (
            flat[offset + j * share : offset + (j + 1) * share].astype(F32) * scale
        )
    return offset + panels * share


def take_bias(flat, offset, out, scale):
    rows = flat[offset : offset + 16].astype(F32) * scale
    out[...] = rows[0:1, : out.shape[1]]


def kernel(
    n_graph, n_rep,
    nodes, cot, live, partner, src_ref, dst_ref, we1, be, we2, wn1, bn, wn2,
    updated_out, dnodes_out, node_flat, edge_flat,
    outgoing, arrived, keygrad, backsend, back, inv,
    x_send, x_recv, b_send, b_recv,
    *group_refs,
):
    me = lax.axis_index("graph")
    rep = lax.axis_index("rep")
    G, B, H = nodes.shape
    R = G * B
    half = G // 2
    E = src_ref.shape[1]
    per = len(group_refs) // 2
    node_group = Reduce(n_graph, n_rep, me, rep, group_refs[:per])
    edge_group = Reduce(n_graph, n_rep, me, rep, group_refs[per:])

    barrier = pltpu.get_barrier_semaphore()
    for d in range(1, n_graph):
        pl.semaphore_signal(barrier, inc=1, device_id={"graph": lax.rem(me + d, n_graph), "rep": rep},
                            device_id_type=pl.DeviceIdType.MESH)
    for d in range(1, n_rep):
        pl.semaphore_signal(barrier, inc=1, device_id={"graph": me, "rep": lax.rem(rep + d, n_rep)},
                            device_id_type=pl.DeviceIdType.MESH)

    def build(p, carry):
        lane = lax.broadcasted_iota(jnp.int32, (16, H), 1)
        row = lax.broadcasted_iota(jnp.int32, (16, H), 0)
        tile = jnp.zeros((16, H), F32)
        for h in range(2):
            first = jnp.int32(0)
            count = jnp.int32(0)
            for g in reversed(range(h * half, (h + 1) * half)):
                hit = partner[0, g] // G == p
                first = jnp.where(hit, g, first)
                count = count + jnp.where(hit, 1, 0)
            second = jnp.minimum(first + 1, G - 1)
            live1 = jnp.where(count > 0, live[0, first], 0)
            live2 = jnp.where(count > 1, live[0, second], 0)
            inv[0, p * 2 + h] = first
            inv[1, p * 2 + h] = count
            outgoing[p, h * GMAX * B : h * GMAX * B + B, :] = nodes[first]
            outgoing[p, h * GMAX * B + B : (h + 1) * GMAX * B, :] = nodes[second]
            bound = jnp.where(lane < B, live1, B + live2)
            bound = jnp.where(row == h, bound, 0)
            tile = tile + jnp.where(lane < bound, 1.0, 0.0)
        outgoing[p, 2 * GMAX * B :, :] = tile.astype(BF16)
        return carry

    lax.fori_loop(0, n_graph, build, 0)
    pl.semaphore_wait(barrier, n_graph + n_rep - 2)

    sends = []

    def exchange(src, dst, s_sem, r_sem):
        waits = []
        for d in range(1, n_graph):
            to = lax.rem(me + d, n_graph)
            frm = lax.rem(me + n_graph - d, n_graph)
            copy = send(src.at[to], dst.at[me], s_sem.at[d], r_sem.at[d], to, rep)
            copy.start()
            sends.append(copy)
            waits.append(send(src.at[to], dst.at[frm], s_sem.at[d], r_sem.at[d], to, rep))
        return waits

    waits = exchange(outgoing, arrived, x_send, x_recv)
    arrived[me] = outgoing[me]

    rows = nodes[...].reshape(R, H)
    row_ids = lax.broadcasted_iota(jnp.int32, (R, E), 0)
    hot = jnp.concatenate(
        [
            jnp.where(row_ids == dst_ref[...], 1.0, 0.0).astype(BF16),
            jnp.where(row_ids == src_ref[...], 1.0, 0.0).astype(BF16),
        ],
        axis=0,
    )
    pre = jnp.concatenate(
        [
            (dot_nn(rows, we1[:H]) + be[...]).astype(BF16),
            dot_nn(rows, we1[H:]).astype(BF16),
        ],
        axis=0,
    )
    summed = dot_tn(hot, pre)
    edge_sig = sigmoid(summed)
    gathered = dot_nn(hot[:R], (summed * edge_sig).astype(BF16)).astype(BF16)
    message = dot_nn(gathered, we2[...]).astype(BF16)
    hidden_pre = dot_nn(rows, wn1[:H]) + dot_nn(message, wn1[H : 2 * H]) + bn[...]
    position = lax.broadcasted_iota(jnp.int32, (B, H), 0)
    mask = jnp.concatenate(
        [jnp.where(position < live[0, g], 1.0, 0.0) for g in range(G)], axis=0
    ) > 0.5
    grad_out = jnp.where(mask, cot[...].reshape(R, H).astype(F32), 0.0).astype(BF16)
    back_hidden = dot_nt(grad_out, wn2[...])

    for copy in waits:
        copy.wait_recv()
    scale = H ** (-0.5)

    def peer(g):
        return partner[0, g] // G

    def keys_of(g):
        off = GMAX * B if g < half else 0
        return arrived[peer(g), off : off + GMAX * B, :]

    def block(values, g):
        return values[g * B : (g + 1) * B]

    score_list, mask_list = [], []
    for g in range(G):
        h = 1 if g < half else 0
        score_list.append(dot_nt(block(rows, g), keys_of(g)))
        tail = arrived[peer(g), 2 * GMAX * B :, :].astype(F32)
        mask_list.append(jnp.broadcast_to(tail[h : h + 1, : GMAX * B], (B, GMAX * B)))
    scores = jnp.concatenate(score_list, axis=0) * scale
    scores = jnp.where(jnp.concatenate(mask_list, axis=0) > 0.5, scores, -jnp.inf)
    powers = jnp.exp(scores - jnp.max(scores, axis=-1, keepdims=True))
    probs = powers / jnp.sum(powers, axis=-1, keepdims=True)
    low = probs.astype(BF16)
    context = jnp.concatenate([dot_nn(block(low, g), keys_of(g)) for g in range(G)], axis=0)
    moved = (rows.astype(F32) - context).astype(BF16)

    hidden_pre = hidden_pre + dot_nn(moved, wn1[2 * H :])
    sig = sigmoid(hidden_pre)
    active = (hidden_pre * sig).astype(BF16)
    grad_hidden = (back_hidden * silu_slope(hidden_pre, sig)).astype(BF16)
    grad_moved = dot_nt(grad_hidden, wn1[2 * H :]).astype(BF16)

    negated = -grad_moved
    grad_probs = jnp.concatenate(
        [dot_nt(block(negated, g), keys_of(g)) for g in range(G)], axis=0
    )
    inner = jnp.sum(probs * grad_probs, axis=-1, keepdims=True)
    grad_scores = (probs * (grad_probs - inner) * scale).astype(BF16)
    for g in range(G):
        left = jnp.concatenate([block(low, g), block(grad_scores, g)], axis=0)
        right = jnp.concatenate([block(negated, g), block(rows, g)], axis=0)
        keygrad[g] = dot_tn(left, right)

    def build_back(p, carry):
        for h in range(2):
            first = inv[0, p * 2 + h]
            count = inv[1, p * 2 + h]
            one = jnp.where(count > 0, 1.0, 0.0)
            two = jnp.where(count > 1, 1.0, 0.0)
            total = keygrad[first] * one + keygrad[jnp.minimum(first + 1, G - 1)] * two
            backsend[p, (1 - h) * GMAX : (2 - h) * GMAX] = total.astype(BF16).reshape(GMAX, B, H)
        return carry

    lax.fori_loop(0, n_graph, build_back, 0)
    back_waits = exchange(backsend, back, b_send, b_recv)
    back[me] = backsend[me]

    full = node_group.full
    pieces = jnp.concatenate(
        [dot_tn(rows, grad_hidden), dot_tn(message, grad_hidden), dot_tn(moved, grad_hidden)], axis=0
    )
    at = put_grad(full, 0, pieces, n_rep)
    at = put_grad(full, at, dot_tn(active, grad_out), n_rep)
    put_bias(full, at, jnp.sum(grad_hidden.astype(F32), axis=0, keepdims=True), n_rep)
    node_group.start_core()

    grad_message = dot_nt(grad_hidden, wn1[H : 2 * H]).astype(BF16)
    grad_gathered = dot_nt(grad_message, we2[...]).astype(BF16)
    edge_grad = (dot_tn(hot[:R], grad_gathered) * silu_slope(summed, edge_sig)).astype(BF16)
    both = dot_nn(hot, edge_grad).astype(BF16)
    grad_target, grad_source = both[:R], both[R:]
    node_group.start_plane()

    full = edge_group.full
    pieces = jnp.concatenate([dot_tn(rows, grad_target), dot_tn(rows, grad_source)], axis=0)
    at = put_grad(full, 0, pieces, n_rep)
    at = put_grad(full, at, dot_tn(gathered, grad_message), n_rep)
    put_bias(full, at, jnp.sum(grad_target.astype(F32), axis=0, keepdims=True), n_rep)
    edge_group.start_core()

    updated = jnp.where(mask, rows.astype(F32) + dot_nn(active, wn2[...]), 0.0)
    updated_out[...] = updated.astype(BF16).reshape(G, B, H)
    total = grad_out.astype(F32) + grad_moved.astype(F32)
    total = total + dot_nt(grad_hidden, wn1[:H])
    total = total + dot_nt(grad_target, we1[:H]) + dot_nt(grad_source, we1[H:])
    total = total + jnp.concatenate(
        [dot_nn(block(grad_scores, g), keys_of(g)) for g in range(G)], axis=0
    )
    edge_group.start_plane()
    for copy in back_waits:
        copy.wait_recv()
    returned = []
    for g in range(G):
        h = 0 if g < half else 1
        same = partner[0, g] == partner[0, g - 1] if g > 0 else False
        place = jnp.where(same, 1, 0)
        returned.append(back[peer(g), h * GMAX + place])
    total = total + jnp.concatenate(returned, axis=0).astype(F32)
    dnodes_out[...] = jnp.where(mask, total, 0.0).astype(BF16).reshape(G, B, H)

    node_group.start_rep()
    edge_group.start_rep()
    node_group.start_gather()
    edge_group.start_gather()
    node_group.start_swap()
    edge_group.start_swap()
    node_group.finish(node_flat)
    edge_group.finish(edge_flat)
    for copy in sends:
        copy.wait_send()
    node_group.drain()
    edge_group.drain()


def unpack(
    grad_scale, updated, dnodes, node_flat, edge_flat,
    updated_out, dnodes_out, oe1, obe, oe2, on1, obn, on2,
):
    updated_out[...] = updated[...]
    dnodes_out[...] = dnodes[...]
    at = take_grad(node_flat, 0, on1, grad_scale)
    at = take_grad(node_flat, at, on2, grad_scale)
    take_bias(node_flat, at, obn, grad_scale)
    at = take_grad(edge_flat, 0, oe1, grad_scale)
    at = take_grad(edge_flat, at, oe2, grad_scale)
    take_bias(edge_flat, at, obe, grad_scale)


def group_scratch(shapes, n_graph, n_rep):
    rows = sum(s[0] // n_rep * (s[1] // LANES) for s in shapes)
    rows = round_up(rows + 16, 16 * n_graph)
    half, ch, chips = rows // 2, rows // n_graph, n_graph // 2
    dma = pltpu.SemaphoreType.DMA
    return [
        pltpu.VMEM((n_rep, rows, LANES), BF16),
        pltpu.VMEM((n_rep, half, LANES), BF16),
        pltpu.VMEM((n_rep, half, LANES), BF16),
        pltpu.VMEM((chips, n_rep, ch, LANES), BF16),
        pltpu.VMEM((n_rep, ch, LANES), BF16),
        pltpu.VMEM((n_rep, ch, LANES), BF16),
        pltpu.VMEM((n_graph, ch, LANES), BF16),
        dma((2,)),
        dma((chips,)),
        dma((chips,)),
        dma((n_rep,)),
        dma((n_rep,)),
        dma((n_graph,)),
        dma((n_graph,)),
    ]


def on_device(
    n_graph, n_rep,
    nodes, cotangent, live, partner_first, partner_size, edge_src, edge_dst,
    w_edge1, b_edge, w_edge2, w_node1, b_node, w_node2,
):
    _, G, B, H = nodes.shape
    FM = w_edge1.shape[1]
    rows_x = 2 * GMAX * B
    dma = pltpu.SemaphoreType.DMA
    vmem = pl.BlockSpec(memory_space=pltpu.VMEM)
    smem = pl.BlockSpec(memory_space=pltpu.SMEM)
    sds = jax.ShapeDtypeStruct

    def share(shape):
        return sds((shape[0] // n_rep,) + tuple(shape[1:]), F32)

    node_scratch = group_scratch([w_node1.shape, w_node2.shape], n_graph, n_rep)
    edge_scratch = group_scratch([w_edge1.shape, w_edge2.shape], n_graph, n_rep)
    parts = pl.pallas_call(
        functools.partial(kernel, n_graph, n_rep),
        out_shape=(
            sds((G, B, H), BF16),
            sds((G, B, H), BF16),
            sds((node_scratch[0].shape[1], LANES), BF16),
            sds((edge_scratch[0].shape[1], LANES), BF16),
        ),
        in_specs=[vmem, vmem, smem, smem] + [vmem] * 8,
        out_specs=(vmem,) * 4,
        scratch_shapes=[
            pltpu.VMEM((n_graph, rows_x + 16, H), BF16),
            pltpu.VMEM((n_graph, rows_x + 16, H), BF16),
            pltpu.VMEM((G, GMAX * B, H), F32),
            pltpu.VMEM((n_graph, 2 * GMAX, B, H), BF16),
            pltpu.VMEM((n_graph, 2 * GMAX, B, H), BF16),
            pltpu.SMEM((2, 2 * n_graph), jnp.int32),
            dma((n_graph,)),
            dma((n_graph,)),
            dma((n_graph,)),
            dma((n_graph,)),
        ]
        + node_scratch
        + edge_scratch,
        compiler_params=pltpu.CompilerParams(
            collective_id=0, has_side_effects=True, vmem_limit_bytes=64 * 1000 * 1000
        ),
    )(
        nodes[0], cotangent[0], live, partner_first, edge_src, edge_dst,
        w_edge1, b_edge.reshape(1, FM), w_edge2, w_node1, b_node.reshape(1, FM), w_node2,
    )
    outs = pl.pallas_call(
        functools.partial(unpack, (n_graph * n_rep * G * B) ** (-0.5)),
        out_shape=(
            sds((G, B, H), BF16),
            sds((G, B, H), BF16),
            share(w_edge1.shape),
            sds((1, FM // n_rep), F32),
            share(w_edge2.shape),
            share(w_node1.shape),
            sds((1, FM // n_rep), F32),
            share(w_node2.shape),
        ),
        in_specs=[vmem] * 4,
        out_specs=(vmem,) * 8,
    )(*parts)
    return (
        outs[0][None],
        outs[1][None],
        outs[2],
        outs[3].reshape(-1),
        outs[4],
        outs[5],
        outs[6].reshape(-1),
        outs[7],
    )


def solution(mesh):
    rows = P("rep", "graph", None, None)
    ints = P("rep", "graph")
    return jax.shard_map(
        functools.partial(on_device, mesh.shape["graph"], mesh.shape["rep"]),
        mesh=mesh,
        in_specs=(rows, rows, ints, ints, ints, ints, ints) + (P(),) * 6,
        out_specs=(
            rows,
            rows,
            P("rep", None),
            P("rep"),
            P("rep", None),
            P("rep", None),
            P("rep"),
            P("rep", None),
        ),
        check_vma=False,
    )
```

profile of v0, /device:TPU:0, one launch (start us, length us, event | category | flops | bytes accessed | tf_op | source)
XLA Modules:
  0.0 48.9 jit_solution(17285959298062433066)
XLA Ops:
  0.6 46.0 %shard_map.179 = (bf16[8,32,256]{2,1,0:T(8,128)(2,1)}, bf16[8,32,256]{2,1,0:T(8,128)(2,1)}, bf16[1152,128]{1,0:T(8,128)(2,1)}, bf16[896,128]{1,0:T(8,128)(2,1)}) custom-call(bf16[8,32,256]{2,1,0:T(8,128)(2,1)} %bitcast.8, bf16[8,32,256]{2,1,0:T(8,128)(2,1)} %bitcast.9, s32[1,8]{1,0:T(1,128)} %live.1, s32[1,8]{1,0:T(1,128)} %partner.1, s32[1,256]{1,0:T(1,128)} %src_ref.1, ...), custom_call_target="tpu_custom_call" | custom-call | tf_op jit(solution)/shard_map/pallas_call | solution.py:443
  46.7 2.2 %shard_map.180 = (bf16[8,32,256]{2,1,0:T(8,128)(2,1)}, bf16[8,32,256]{2,1,0:T(8,128)(2,1)}, f32[128,512]{1,0:T(8,128)}, f32[1,128]{1,0:T(1,128)}, f32[128,256]{1...) custom-call(bf16[8,32,256]{2,1,0:T(8,128)(2,1)} %get-tuple-element.20.updated, ...), custom_call_target="tpu_custom_call" | custom-call | tf_op jit(solution)/shard_map/pallas_call | solution.py:474
where the time goes:
time: 49.1 us; the launch traced here: 48.9 us
  Pallas kernels  48.2 us (98%)
  between operations  0.65 us (1%)
    pallas_call x1, Pallas kernels, on_device(): pl.pallas_call(functools.partial(kernel, n_graph, n_rep), out_shape=(sds(...  46 us
    pallas_call x1, Pallas kernels, on_device(): pl.pallas_call(functools.partial(unpack, (n_graph * n_rep * G * B) ** (-0...  2.2 us

commit v1 on v0

v1 whole, which is shorter than its diff:
```python
import functools

import jax
import jax.numpy as jnp
from jax import lax
from jax.experimental import pallas as pl
from jax.experimental.pallas import tpu as pltpu
from jax.sharding import PartitionSpec as P

GMAX = 2
LANES = 128
F32 = jnp.float32
BF16 = jnp.bfloat16


def dot_nn(a, b):
    return lax.dot_general(a, b, (((1,), (0,)), ((), ())), preferred_element_type=F32)


def dot_nt(a, b):
    return lax.dot_general(a, b, (((1,), (1,)), ((), ())), preferred_element_type=F32)


def dot_tn(a, b):
    return lax.dot_general(a, b, (((0,), (0,)), ((), ())), preferred_element_type=F32)


def sigmoid(v):
    return 1.0 / (1.0 + jnp.exp(-v))


def silu_slope(v, s):
    return s * (1.0 + v * (1.0 - s))


def round_up(value, unit):
    return -(-value // unit) * unit


def send(src, dst, send_sem, recv_sem, graph, rep):
    return pltpu.make_async_remote_copy(
        src_ref=src,
        dst_ref=dst,
        send_sem=send_sem,
        recv_sem=recv_sem,
        device_id={"graph": graph, "rep": rep},
        device_id_type=pl.DeviceIdType.MESH,
    )


class Group:
    def __init__(self, n_graph, n_rep, me, rep, plane_first, refs):
        self.n, self.r, self.me, self.rep = n_graph, n_rep, me, rep
        (self.full, self.r1, self.b, self.r2, self.got,
         self.s1, self.v1, self.s2, self.v2, self.s3, self.v3) = refs
        self.plane_first = plane_first
        self.chips = n_graph // 2
        self.core = lax.rem(me, 2)
        self.chip = lax.div(me, 2)
        self.ch = self.full.shape[1] // self.chips
        self.sends = []
        self.firsts = []

    def go(self, copy):
        copy.start()
        self.sends.append(copy)
        return copy

    def rows(self, q):
        return pl.ds(pl.multiple_of(q * self.ch, 16), self.ch)

    def over_plane(self, source, landing, s, v):
        copies = []
        for d in range(1, self.chips):
            q = lax.rem(self.chip + d, self.chips)
            copies.append(self.go(send(source(q), landing.at[d], s.at[d], v.at[d],
                                       q * 2 + self.core, self.rep)))
        return copies

    def over_rep(self, source, landing, s, v, at=0):
        copies = []
        for d in range(1, self.r):
            z = lax.rem(self.rep + d, self.r)
            copies.append(self.go(send(source(z), landing(d), s.at[at + d], v.at[at + d], self.me, z)))
        return copies

    def first_plane(self):
        self.firsts = self.over_plane(lambda q: self.full.at[:, self.rows(q), :], self.r1, self.s1, self.v1)

    def first_rep(self, part, start, stop):
        self.firsts += self.over_rep(lambda z: self.full.at[z, start:stop],
                                     lambda d: self.r1.at[d, start:stop], self.s1, self.v1, part * self.r)

    def second(self):
        for copy in self.firsts:
            copy.wait_recv()
        if self.plane_first:
            total = self.full[:, self.rows(self.chip), :].astype(F32)
            count = self.chips
        else:
            total = self.full[self.rep].astype(F32)
            count = self.r
        for d in range(1, count):
            total = total + self.r1[d].astype(F32)
        self.b[...] = total.astype(BF16)
        if self.plane_first:
            self.seconds = self.over_rep(lambda z: self.b.at[z], lambda d: self.r2.at[d], self.s2, self.v2)
        else:
            self.seconds = self.over_plane(lambda q: self.b.at[self.rows(q)], self.r2, self.s2, self.v2)

    def gather(self):
        if self.plane_first:
            total = self.b[self.rep].astype(F32)
            count = self.r
        else:
            total = self.b[self.rows(self.chip), :].astype(F32)
            count = self.chips
        for copy in self.seconds:
            copy.wait_recv()
        for d in range(1, count):
            total = total + self.r2[d].astype(F32)
        place = self.core * self.chips + self.chip
        self.got[place] = total.astype(BF16)
        self.thirds = []
        for d in range(1, self.chips):
            to = lax.rem(self.chip + d, self.chips) * 2 + self.core
            frm = self.core * self.chips + lax.rem(self.chip + self.chips - d, self.chips)
            self.go(send(self.got.at[place], self.got.at[place], self.s3.at[d], self.v3.at[d], to, self.rep))
            self.thirds.append(send(self.got.at[frm], self.got.at[frm], self.s3.at[d], self.v3.at[d],
                                    to, self.rep))

    def swap(self):
        for copy in self.thirds:
            copy.wait_recv()
        other = 1 - self.core
        mine = self.got.at[pl.ds(self.core * self.chips, self.chips)]
        theirs = self.got.at[pl.ds(other * self.chips, self.chips)]
        to = self.chip * 2 + other
        self.go(send(mine, mine, self.s3.at[0], self.v3.at[0], to, self.rep))
        self.last = send(theirs, theirs, self.s3.at[0], self.v3.at[0], to, self.rep)

    def finish(self, out):
        self.last.wait_recv()
        out[...] = self.got[...].reshape(self.n * self.ch, LANES)

    def drain(self):
        for copy in self.sends:
            copy.wait_send()


def put_grad(full, offset, grad, n_rep):
    share = grad.shape[0] // n_rep
    low = grad.astype(BF16)
    for j in range(grad.shape[1] // LANES):
        full[:, offset + j * share : offset + (j + 1) * share, :] = low[
            :, j * LANES : (j + 1) * LANES
        ].reshape(n_rep, share, LANES)


def half_rows(shape, n_rep):
    return shape[0] // n_rep * (shape[1] // 2 // LANES)


def take_grad(flat, offset, out, scale):
    share = out.shape[0]
    panels = out.shape[1] // 2 // LANES
    rows = flat.shape[0] // 2
    for c in range(2):
        for j in range(panels):
            at = c * rows + offset + j * share
            col = (c * panels + j) * LANES
            out[:, col : col + LANES] = flat[at : at + share].astype(F32) * scale


def kernel(
    n_graph, n_rep,
    nodes, live, partner, psize, src_ref, dst_ref,
    cot_in, we1_in, be_in, we2_in, wn1_in, bn_in, wn2_in,
    updated_out, dnodes_out, flat_a, flat_b, flat_c, bias_out,
    cot, we1, be, we2, wn1, bn, wn2,
    outgoing, arrived, livebox, livefrom, keygrad, backsend, back, inv,
    msg_f, moved_f, gh_f, act_f, go_f, gat_f, gm_f, gts_f,
    nodes_s, msg_s, moved_s, gh_s, act_s, go_s, gat_s, gm_s, gts_s,
    bias_f, bias_g, bias_m, bias_r,
    load_sem, x_send, x_recv, l_send, l_recv, b_send, b_recv, sib_send, sib_recv,
    c_send, c_recv, d_send, d_recv,
    *group_refs,
):
    me = lax.axis_index("graph")
    rep = lax.axis_index("rep")
    core = lax.rem(me, 2)
    other = 1 - core
    sibling = me + other - core
    G, B, H = nodes.shape
    R = G * B
    half = G // 2
    E = src_ref.shape[1]
    FM = wn1.shape[1]
    per = len(group_refs) // 3
    ga = Group(n_graph, n_rep, me, rep, True, group_refs[:per])
    gb = Group(n_graph, n_rep, me, rep, True, group_refs[per : 2 * per])
    gc = Group(n_graph, n_rep, me, rep, False, group_refs[2 * per :])

    barrier = pltpu.get_barrier_semaphore()
    for d in range(1, n_graph):
        pl.semaphore_signal(barrier, inc=1, device_id={"graph": lax.rem(me + d, n_graph), "rep": rep},
                            device_id_type=pl.DeviceIdType.MESH)
    for d in range(1, n_rep):
        pl.semaphore_signal(barrier, inc=1, device_id={"graph": me, "rep": lax.rem(rep + d, n_rep)},
                            device_id_type=pl.DeviceIdType.MESH)
    loads = []
    pairs = ((we1_in, we1), (be_in, be), (we2_in, we2), (wn1_in, wn1), (bn_in, bn), (cot_in, cot), (wn2_in, wn2))
    for i, (a, b) in enumerate(pairs):
        copy = pltpu.make_async_copy(a, b, load_sem.at[i])
        copy.start()
        loads.append(copy)

    owner = [lax.div(partner[0, g], G) for g in range(G)]
    for g in range(G):
        livebox[g : g + 1, :] = jnp.full((1, LANES), live[0, g].astype(F32))
    livefrom[me] = livebox[...]

    def build(p):
        for h in range(2):
            first = jnp.int32(0)
            count = jnp.int32(0)
            for g in reversed(range(h * half, (h + 1) * half)):
                hit = owner[g] == p
                first = jnp.where(hit, g, first)
                count = count + jnp.where(hit, 1, 0)
            inv[0, p * 2 + h] = first
            inv[1, p * 2 + h] = count
            outgoing[p, h * GMAX * B : h * GMAX * B + B, :] = nodes[first]
            outgoing[p, h * GMAX * B + B : (h + 1) * GMAX * B, :] = nodes[jnp.minimum(first + 1, G - 1)]

    pl.semaphore_wait(barrier, n_graph + n_rep - 2)

    sends = []
    live_waits = []
    for d in range(1, n_graph):
        to = lax.rem(me + d, n_graph)
        frm = lax.rem(me + n_graph - d, n_graph)
        copy = send(livebox, livefrom.at[me], l_send.at[d], l_recv.at[d], to, rep)
        copy.start()
        sends.append(copy)
        live_waits.append(send(livebox, livefrom.at[frm], l_send.at[d], l_recv.at[d], to, rep))

    def ship(d, carry):
        to = lax.rem(me + d, n_graph)
        build(to)
        send(outgoing.at[to], arrived.at[me], x_send.at[d], x_recv.at[d], to, rep).start()
        return carry

    lax.fori_loop(1, n_graph, ship, 0)
    key_waits = []
    for d in range(1, n_graph):
        to = lax.rem(me + d, n_graph)
        frm = lax.rem(me + n_graph - d, n_graph)
        sends.append(send(outgoing.at[to], arrived.at[me], x_send.at[d], x_recv.at[d], to, rep))
        key_waits.append(send(outgoing.at[to], arrived.at[frm], x_send.at[d], x_recv.at[d], to, rep))
    build(me)
    arrived[me] = outgoing[me]

    def share(i, src, dst):
        copy = send(src, dst, sib_send.at[i], sib_recv.at[i], sibling, rep)
        copy.start()
        sends.append(copy)
        return copy

    share_nodes = share(0, nodes, nodes_s)

    rows = nodes[...].reshape(R, H)
    row_ids = lax.broadcasted_iota(jnp.int32, (R, E), 0)
    hot = jnp.concatenate(
        [
            jnp.where(row_ids == dst_ref[...], 1.0, 0.0).astype(BF16),
            jnp.where(row_ids == src_ref[...], 1.0, 0.0).astype(BF16),
        ],
        axis=0,
    )
    loads[0].wait()
    loads[1].wait()
    pre = jnp.concatenate(
        [
            (dot_nn(rows, we1[:H]) + be[...]).astype(BF16),
            dot_nn(rows, we1[H:]).astype(BF16),
        ],
        axis=0,
    )
    summed = dot_tn(hot, pre)
    edge_sig = sigmoid(summed)
    gathered = dot_nn(hot[:R], (summed * edge_sig).astype(BF16)).astype(BF16)
    gat_f[...] = gathered
    share_gat = share(1, gat_f, gat_s)
    loads[2].wait()
    message = dot_nn(gathered, we2[...]).astype(BF16)
    msg_f[...] = message
    share_msg = share(2, msg_f, msg_s)
    loads[3].wait()
    loads[4].wait()
    hidden_pre = dot_nn(rows, wn1[:H]) + dot_nn(message, wn1[H : 2 * H]) + bn[...]
    position = lax.broadcasted_iota(jnp.int32, (B, H), 0)
    mask = jnp.concatenate(
        [jnp.where(position < live[0, g], 1.0, 0.0) for g in range(G)], axis=0
    ) > 0.5
    loads[5].wait()
    loads[6].wait()
    grad_out = jnp.where(mask, cot[...].reshape(R, H).astype(F32), 0.0).astype(BF16)
    for c in range(2):
        go_f[c] = grad_out[:, c * (H // 2) : (c + 1) * (H // 2)]
    share_go = share(3, go_f.at[other], go_s)
    back_hidden = dot_nt(grad_out, wn2[...])

    for copy in live_waits + key_waits:
        copy.wait_recv()
    scale = H ** (-0.5)

    def keys_of(g):
        off = GMAX * B if g < half else 0
        return arrived[owner[g], off : off + GMAX * B, :]

    def block(values, g):
        return values[g * B : (g + 1) * B]

    lane = lax.broadcasted_iota(jnp.int32, (1, LANES), 1).astype(F32)
    score_list, bound_list = [], []
    for g in range(G):
        score_list.append(dot_nt(block(rows, g), keys_of(g)))
        at = partner[0, g] - owner[g] * G
        one = livefrom[owner[g], pl.ds(at, 1), :]
        two = livefrom[owner[g], pl.ds(jnp.minimum(at + 1, G - 1), 1), :]
        two = two * jnp.where(psize[0, g] > 1, 1.0, 0.0)
        bound = jnp.where(lane < B, one, B + two) - lane
        bound_list.append(jnp.broadcast_to(bound[:, : GMAX * B], (B, GMAX * B)))
    scores = jnp.concatenate(score_list, axis=0) * scale
    scores = jnp.where(jnp.concatenate(bound_list, axis=0) > 0.5, scores, -jnp.inf)
    powers = jnp.exp(scores - jnp.max(scores, axis=-1, keepdims=True))
    probs = powers / jnp.sum(powers, axis=-1, keepdims=True)
    low = probs.astype(BF16)
    context = jnp.concatenate([dot_nn(block(low, g), keys_of(g)) for g in range(G)], axis=0)
    moved = (rows.astype(F32) - context).astype(BF16)
    moved_f[...] = moved
    share_moved = share(4, moved_f, moved_s)

    hidden_pre = hidden_pre + dot_nn(moved, wn1[2 * H :])
    sig = sigmoid(hidden_pre)
    grad_hidden = (back_hidden * silu_slope(hidden_pre, sig)).astype(BF16)
    for c in range(2):
        gh_f[c] = grad_hidden[:, c * (FM // 2) : (c + 1) * (FM // 2)]
    share_gh = share(5, gh_f.at[other], gh_s)
    active = (hidden_pre * sig).astype(BF16)
    act_f[...] = active
    share_act = share(6, act_f, act_s)

    grad_message = dot_nt(grad_hidden, wn1[H : 2 * H]).astype(BF16)
    for c in range(2):
        gm_f[c] = grad_message[:, c * (H // 2) : (c + 1) * (H // 2)]
    share_gm = share(7, gm_f.at[other], gm_s)
    grad_gathered = dot_nt(grad_message, we2[...]).astype(BF16)
    edge_grad = (dot_tn(hot[:R], grad_gathered) * silu_slope(summed, edge_sig)).astype(BF16)
    both = dot_nn(hot, edge_grad).astype(BF16)
    for c in range(2):
        gts_f[c] = both[:, c * (FM // 2) : (c + 1) * (FM // 2)]
    share_gts = share(8, gts_f.at[other], gts_s)
    grad_target, grad_source = both[:R], both[R:]

    def two_cores(mine, theirs):
        return jnp.concatenate([mine, theirs], axis=0)

    for copy in (share_nodes, share_msg, share_moved, share_gh):
        copy.wait_recv()
    rows2 = two_cores(rows, nodes_s[...].reshape(R, H))
    gh2 = two_cores(gh_f[core], gh_s[...])
    pieces = jnp.concatenate(
        [dot_tn(rows2, gh2), dot_tn(two_cores(message, msg_s[...]), gh2),
         dot_tn(two_cores(moved, moved_s[...]), gh2)],
        axis=0,
    )
    put_grad(ga.full, 0, pieces, n_rep)
    ga.first_plane()

    for copy in (share_go, share_act):
        copy.wait_recv()
    piece = dot_tn(two_cores(active, act_s[...]), two_cores(go_f[core], go_s[...]))
    put_grad(gc.full, 0, piece, n_rep)
    cut = piece.shape[0] // n_rep * (piece.shape[1] // LANES)
    gc.first_rep(0, 0, cut)

    for copy in (share_gat, share_gm):
        copy.wait_recv()
    piece = dot_tn(two_cores(gathered, gat_s[...]), two_cores(gm_f[core], gm_s[...]))
    put_grad(gc.full, cut, piece, n_rep)
    gc.first_rep(1, cut, gc.full.shape[1])

    share_gts.wait_recv()
    mine, theirs = gts_f[core], gts_s[...]
    pieces = jnp.concatenate(
        [dot_tn(rows2, two_cores(mine[:R], theirs[:R])), dot_tn(rows2, two_cores(mine[R:], theirs[R:]))],
        axis=0,
    )
    put_grad(gb.full, 0, pieces, n_rep)
    gb.first_plane()

    width = FM // n_rep
    sums = (jnp.sum(grad_hidden.astype(F32), axis=0, keepdims=True),
            jnp.sum(grad_target.astype(F32), axis=0, keepdims=True))
    for i in range(2):
        for z in range(n_rep):
            row = sums[i][:, z * width : (z + 1) * width]
            if width < LANES:
                row = jnp.concatenate([row, jnp.zeros((1, LANES - width), F32)], axis=1)
            bias_f[i * n_rep + z : i * n_rep + z + 1, :] = row
    bias_g[me] = bias_f[...]
    bias_waits = []
    for d in range(1, n_graph):
        to = lax.rem(me + d, n_graph)
        frm = lax.rem(me + n_graph - d, n_graph)
        copy = send(bias_f, bias_g.at[me], c_send.at[d], c_recv.at[d], to, rep)
        copy.start()
        sends.append(copy)
        bias_waits.append(send(bias_f, bias_g.at[frm], c_send.at[d], c_recv.at[d], to, rep))

    grad_moved = dot_nt(grad_hidden, wn1[2 * H :]).astype(BF16)
    negated = -grad_moved
    grad_probs = jnp.concatenate(
        [dot_nt(block(negated, g), keys_of(g)) for g in range(G)], axis=0
    )
    inner = jnp.sum(probs * grad_probs, axis=-1, keepdims=True)
    grad_scores = (probs * (grad_probs - inner) * scale).astype(BF16)
    for g in range(G):
        left = jnp.concatenate([block(low, g), block(grad_scores, g)], axis=0)
        right = jnp.concatenate([block(negated, g), block(rows, g)], axis=0)
        keygrad[g] = dot_tn(left, right)

    def ship_back(d, carry):
        to = lax.rem(me + d, n_graph)
        for h in range(2):
            first = inv[0, to * 2 + h]
            count = inv[1, to * 2 + h]
            one = jnp.where(count > 0, 1.0, 0.0)
            two = jnp.where(count > 1, 1.0, 0.0)
            total = keygrad[first] * one + keygrad[jnp.minimum(first + 1, G - 1)] * two
            backsend[to, (1 - h) * GMAX : (2 - h) * GMAX] = total.astype(BF16).reshape(GMAX, B, H)
        return carry

    lax.fori_loop(0, n_graph, ship_back, 0)
    back[me] = backsend[me]
    back_waits = []
    for d in range(1, n_graph):
        to = lax.rem(me + d, n_graph)
        frm = lax.rem(me + n_graph - d, n_graph)
        copy = send(backsend.at[to], back.at[me], b_send.at[d], b_recv.at[d], to, rep)
        copy.start()
        sends.append(copy)
        back_waits.append(send(backsend.at[to], back.at[frm], b_send.at[d], b_recv.at[d], to, rep))

    updated = jnp.where(mask, rows.astype(F32) + dot_nn(active, wn2[...]), 0.0)
    updated_out[...] = updated.astype(BF16).reshape(G, B, H)
    total = grad_out.astype(F32) + grad_moved.astype(F32)
    total = total + dot_nt(grad_hidden, wn1[:H])
    total = total + dot_nt(grad_target, we1[:H]) + dot_nt(grad_source, we1[H:])
    total = total + jnp.concatenate(
        [dot_nn(block(grad_scores, g), keys_of(g)) for g in range(G)], axis=0
    )

    ga.second()
    for copy in bias_waits:
        copy.wait_recv()
    summed_bias = bias_g[0]
    for i in range(1, n_graph):
        summed_bias = summed_bias + bias_g[i]
    bias_m[...] = summed_bias
    bias_r[rep] = summed_bias
    bias_waits = []
    for d in range(1, n_rep):
        to = lax.rem(rep + d, n_rep)
        frm = lax.rem(rep + n_rep - d, n_rep)
        copy = send(bias_m, bias_r.at[rep], d_send.at[d], d_recv.at[d], me, to)
        copy.start()
        sends.append(copy)
        bias_waits.append(send(bias_m, bias_r.at[frm], d_send.at[d], d_recv.at[d], me, to))
    gc.second()
    gb.second()
    for copy in back_waits:
        copy.wait_recv()
    returned = []
    for g in range(G):
        h = 0 if g < half else 1
        same = partner[0, g] == partner[0, g - 1] if g > 0 else False
        place = jnp.where(same, 1, 0)
        returned.append(back[owner[g], h * GMAX + place])
    total = total + jnp.concatenate(returned, axis=0).astype(F32)
    dnodes_out[...] = jnp.where(mask, total, 0.0).astype(BF16).reshape(G, B, H)
    for copy in bias_waits:
        copy.wait_recv()
    for i in range(2):
        row = bias_r[0, pl.ds(i * n_rep + rep, 1), :]
        for z in range(1, n_rep):
            row = row + bias_r[z, pl.ds(i * n_rep + rep, 1), :]
        bias_out[i : i + 1, :] = row

    ga.gather()
    gb.gather()
    gc.gather()
    ga.swap()
    gb.swap()
    gc.swap()
    ga.finish(flat_a)
    gb.finish(flat_b)
    gc.finish(flat_c)
    for copy in sends:
        copy.wait_send()
    for group in (ga, gb, gc):
        group.drain()


def unpack(
    grad_scale, updated, dnodes, flat_a, flat_b, flat_c, bias,
    updated_out, dnodes_out, oe1, obe, oe2, on1, obn, on2,
):
    updated_out[...] = updated[...]
    dnodes_out[...] = dnodes[...]
    take_grad(flat_a, 0, on1, grad_scale)
    take_grad(flat_b, 0, oe1, grad_scale)
    take_grad(flat_c, 0, on2, grad_scale)
    take_grad(flat_c, on2.shape[0] * (on2.shape[1] // 2 // LANES), oe2, grad_scale)
    obn[...] = bias[0:1, : obn.shape[1]] * grad_scale
    obe[...] = bias[1:2, : obe.shape[1]] * grad_scale


def group_scratch(shapes, n_graph, n_rep, plane_first):
    chips = n_graph // 2
    rows = round_up(sum(half_rows(s, n_rep) for s in shapes), 16 * chips)
    ch = rows // chips
    dma = pltpu.SemaphoreType.DMA
    plane = (chips, n_rep, ch, LANES)
    if plane_first:
        middle = [plane, (n_rep, ch, LANES), (n_rep, ch, LANES)]
        first, second = chips, n_rep
    else:
        middle = [(n_rep, rows, LANES), (rows, LANES), (chips, ch, LANES)]
        first, second = len(shapes) * n_rep, chips
    return [pltpu.VMEM((n_rep, rows, LANES), BF16)] + [pltpu.VMEM(s, BF16) for s in middle] + [
        pltpu.VMEM((n_graph, ch, LANES), BF16),
        dma((first,)), dma((first,)), dma((second,)), dma((second,)), dma((n_graph,)), dma((n_graph,)),
    ]


def on_device(
    n_graph, n_rep,
    nodes, cotangent, live, partner_first, partner_size, edge_src, edge_dst,
    w_edge1, b_edge, w_edge2, w_node1, b_node, w_node2,
):
    _, G, B, H = nodes.shape
    FM = w_edge1.shape[1]
    R = G * B
    dma = pltpu.SemaphoreType.DMA
    vmem = pl.BlockSpec(memory_space=pltpu.VMEM)
    smem = pl.BlockSpec(memory_space=pltpu.SMEM)
    hbm = pl.BlockSpec(memory_space=pl.ANY)
    sds = jax.ShapeDtypeStruct

    def share(shape):
        return sds((shape[0] // n_rep,) + tuple(shape[1:]), F32)

    groups = [
        group_scratch([w_node1.shape], n_graph, n_rep, True),
        group_scratch([w_edge1.shape], n_graph, n_rep, True),
        group_scratch([w_node2.shape, w_edge2.shape], n_graph, n_rep, False),
    ]
    flats = tuple(sds((2 * g[0].shape[1], LANES), BF16) for g in groups)
    weights = [cotangent[0], w_edge1, b_edge.reshape(1, FM), w_edge2, w_node1, b_node.reshape(1, FM), w_node2]

    def wide(*shape):
        return pltpu.VMEM(shape, F32)

    def bf(*shape):
        return pltpu.VMEM(shape, BF16)

    parts = pl.pallas_call(
        functools.partial(kernel, n_graph, n_rep),
        out_shape=(sds((G, B, H), BF16), sds((G, B, H), BF16)) + flats + (sds((2, LANES), F32),),
        in_specs=[vmem, smem, smem, smem, vmem, vmem] + [hbm] * 7,
        out_specs=(vmem,) * 6,
        scratch_shapes=[pltpu.VMEM(w.shape, w.dtype) for w in weights]
        + [
            bf(n_graph, 2 * GMAX * B, H),
            bf(n_graph, 2 * GMAX * B, H),
            wide(G, LANES),
            wide(n_graph, G, LANES),
            wide(G, GMAX * B, H),
            bf(n_graph, 2 * GMAX, B, H),
            bf(n_graph, 2 * GMAX, B, H),
            pltpu.SMEM((2, 2 * n_graph), jnp.int32),
            bf(R, H), bf(R, H), bf(2, R, FM // 2), bf(R, FM), bf(2, R, H // 2), bf(R, FM),
            bf(2, R, H // 2), bf(2, 2 * R, FM // 2),
            bf(G, B, H), bf(R, H), bf(R, H), bf(R, FM // 2), bf(R, FM), bf(R, H // 2), bf(R, FM),
            bf(R, H // 2), bf(2 * R, FM // 2),
            wide(2 * n_rep, LANES), wide(n_graph, 2 * n_rep, LANES), wide(2 * n_rep, LANES),
            wide(n_rep, 2 * n_rep, LANES),
            dma((7,)),
            dma((n_graph,)), dma((n_graph,)), dma((n_graph,)), dma((n_graph,)),
            dma((n_graph,)), dma((n_graph,)), dma((9,)), dma((9,)),
            dma((n_graph,)), dma((n_graph,)), dma((n_rep,)), dma((n_rep,)),
        ]
        + sum(groups, []),
        compiler_params=pltpu.CompilerParams(
            collective_id=0, has_side_effects=True, vmem_limit_bytes=64 * 1000 * 1000
        ),
    )(nodes[0], live, partner_first, partner_size, edge_src, edge_dst, *weights)
    outs = pl.pallas_call(
        functools.partial(unpack, (n_graph * n_rep * G * B) ** (-0.5)),
        out_shape=(
            sds((G, B, H), BF16),
            sds((G, B, H), BF16),
            share(w_edge1.shape),
            sds((1, FM // n_rep), F32),
            share(w_edge2.shape),
            share(w_node1.shape),
            sds((1, FM // n_rep), F32),
            share(w_node2.shape),
        ),
        in_specs=[vmem] * 6,
        out_specs=(vmem,) * 8,
    )(*parts)
    return (
        outs[0][None],
        outs[1][None],
        outs[2],
        outs[3].reshape(-1),
        outs[4],
        outs[5],
        outs[6].reshape(-1),
        outs[7],
    )


def solution(mesh):
    rows = P("rep", "graph", None, None)
    ints = P("rep", "graph")
    return jax.shard_map(
        functools.partial(on_device, mesh.shape["graph"], mesh.shape["rep"]),
        mesh=mesh,
        in_specs=(rows, rows, ints, ints, ints, ints, ints) + (P(),) * 6,
        out_specs=(
            rows,
            rows,
            P("rep", None),
            P("rep"),
            P("rep", None),
            P("rep", None),
            P("rep"),
            P("rep", None),
        ),
        check_vma=False,
    )
```

time: 49.1 us -> 42.9 us (0.87)
  Pallas kernels: 48.2 us -> 42.1 us
    pallas_call x1, Pallas kernels: 46 us -> 39.8 us  [on_device(): pl.pallas_call(functools.partial(kernel, n_graph, n_rep), out_shape=(sds(...]
where the time goes in v1:
time: 42.9 us; the launch traced here: 42.7 us
  Pallas kernels  42.1 us (98%)
  between operations  0.65 us (2%)
    pallas_call x1, Pallas kernels, on_device(): pl.pallas_call(functools.partial(kernel, n_graph, n_rep), out_shape=(sds(...  39.8 us
    pallas_call x1, Pallas kernels, on_device(): pl.pallas_call(functools.partial(unpack, (n_graph * n_rep * G * B) ** (-0...  2.23 us

profile of v1, /device:TPU:0, one launch (start us, length us, event | category | flops | bytes accessed | tf_op | source)
XLA Modules:
  0.0 42.7 jit_solution(6042542726866347362)
XLA Ops:
  0.6 39.8 %shard_map.188 = (bf16[8,32,256]{2,1,0:T(8,128)(2,1)}, bf16[8,32,256]{2,1,0:T(8,128)(2,1)}, bf16[768,128]{1,0:T(8,128)(2,1)}, bf16[512,128]{1,0:T(8,128)(2,1)}, ...) custom-call(bf16[8,32,256]{2,1,0:T(8,128)(2,1)} %bitcast.8, s32[1,8]{1,0:T(1,128)} %live.1, s32[1,8]{1,0:T(1,128)} %partner.1, ...), custom_call_target="tpu_custom_call" | custom-call | tf_op jit(solution)/shard_map/pallas_call | solution.py:580
  40.5 2.2 %shard_map.189 = (bf16[8,32,256]{2,1,0:T(8,128)(2,1)}, bf16[8,32,256]{2,1,0:T(8,128)(2,1)}, f32[128,512]{1,0:T(8,128)}, f32[1,128]{1,0:T(1,128)}, f32[128,256]{1...) custom-call(bf16[8,32,256]{2,1,0:T(8,128)(2,1)} %get-tuple-element.22.updated, ...), custom_call_target="tpu_custom_call" | custom-call | tf_op jit(solution)/shard_map/pallas_call | solution.py:611

commit v2 on v1

--- a/solution.py
+++ b/solution.py
@@ -1,4 +1,5 @@
 import functools
+import math
 
 import jax
 import jax.numpy as jnp
@@ -26,7 +27,7 @@
 
 
 def sigmoid(v):
-    return 1.0 / (1.0 + jnp.exp(-v))
+    return 0.5 * jnp.tanh(0.5 * v) + 0.5
 
 
 def silu_slope(v, s):
@@ -174,18 +175,20 @@
 
 def kernel(
     n_graph, n_rep,
-    nodes, live, partner, psize, src_ref, dst_ref,
-    cot_in, we1_in, be_in, we2_in, wn1_in, bn_in, wn2_in,
-    updated_out, dnodes_out, flat_a, flat_b, flat_c, bias_out,
-    cot, we1, be, we2, wn1, bn, wn2,
-    outgoing, arrived, livebox, livefrom, keygrad, backsend, back, inv,
-    msg_f, moved_f, gh_f, act_f, go_f, gat_f, gm_f, gts_f,
-    nodes_s, msg_s, moved_s, gh_s, act_s, go_s, gat_s, gm_s, gts_s,
-    bias_f, bias_g, bias_m, bias_r,
-    load_sem, x_send, x_recv, l_send, l_recv, b_send, b_recv, sib_send, sib_recv,
-    c_send, c_recv, d_send, d_recv,
-    *group_refs,
+    *refs
 ):
+    ins, outs, held, rest = refs[:13], refs[13:19], refs[19:32], refs[32:]
+    live, partner, psize, nodes, src_ref, dst_ref, we1, be, we2, wn1, bn, cot, wn2 = held
+    updated_out, dnodes_out, flat_a, flat_b, flat_c, bias_out = outs
+    (outgoing, arrived_low, arrived_high, livebox, livefrom, keygrad, backsend, back, inv,
+     msg_f, moved_f, gh_f, act_f, go_f, gat_f, gm_f, gts_f,
+     nodes_s, msg_s, moved_s, gh_s, act_s, go_s, gat_s, gm_s, gts_s,
+     nodes_t, msg_t, gat_t,
+     bias_f, bias_g, bias_m, bias_r,
+     load_sem, x_send, x_recv, l_send, l_recv, b_send, b_recv, sib_send, sib_recv,
+     c_send, c_recv, d_send, d_recv) = rest[:46]
+    group_refs = rest[46:]
+    arrived = (arrived_low, arrived_high)
     me = lax.axis_index("graph")
     rep = lax.axis_index("rep")
     core = lax.rem(me, 2)
@@ -201,6 +204,11 @@
     gb = Group(n_graph, n_rep, me, rep, True, group_refs[per : 2 * per])
     gc = Group(n_graph, n_rep, me, rep, False, group_refs[2 * per :])
 
+    loads = []
+    for i, (a, b) in enumerate(zip(ins, held)):
+        copy = pltpu.make_async_copy(a, b, load_sem.at[i])
+        copy.start()
+        loads.append(copy)
     barrier = pltpu.get_barrier_semaphore()
     for d in range(1, n_graph):
         pl.semaphore_signal(barrier, inc=1, device_id={"graph": lax.rem(me + d, n_graph), "rep": rep},
@@ -208,30 +216,24 @@
     for d in range(1, n_rep):
         pl.semaphore_signal(barrier, inc=1, device_id={"graph": me, "rep": lax.rem(rep + d, n_rep)},
                             device_id_type=pl.DeviceIdType.MESH)
-    loads = []
-    pairs = ((we1_in, we1), (be_in, be), (we2_in, we2), (wn1_in, wn1), (bn_in, bn), (cot_in, cot), (wn2_in, wn2))
-    for i, (a, b) in enumerate(pairs):
-        copy = pltpu.make_async_copy(a, b, load_sem.at[i])
-        copy.start()
-        loads.append(copy)
-
+    for copy in loads[:4]:
+        copy.wait()
     owner = [lax.div(partner[0, g], G) for g in range(G)]
     for g in range(G):
         livebox[g : g + 1, :] = jnp.full((1, LANES), live[0, g].astype(F32))
     livefrom[me] = livebox[...]
 
-    def build(p):
-        for h in range(2):
-            first = jnp.int32(0)
-            count = jnp.int32(0)
-            for g in reversed(range(h * half, (h + 1) * half)):
-                hit = owner[g] == p
-                first = jnp.where(hit, g, first)
-                count = count + jnp.where(hit, 1, 0)
-            inv[0, p * 2 + h] = first
-            inv[1, p * 2 + h] = count
-            outgoing[p, h * GMAX * B : h * GMAX * B + B, :] = nodes[first]
-            outgoing[p, h * GMAX * B + B : (h + 1) * GMAX * B, :] = nodes[jnp.minimum(first + 1, G - 1)]
+    def build(p, h):
+        first = jnp.int32(0)
+        count = jnp.int32(0)
+        for g in reversed(range(h * half, (h + 1) * half)):
+            hit = owner[g] == p
+            first = jnp.where(hit, g, first)
+            count = count + jnp.where(hit, 1, 0)
+        inv[0, p * 2 + h] = first
+        inv[1, p * 2 + h] = count
+        outgoing[p, h, :B, :] = nodes[first]
+        outgoing[p, h, B:, :] = nodes[jnp.minimum(first + 1, G - 1)]
 
     pl.semaphore_wait(barrier, n_graph + n_rep - 2)
 
@@ -245,21 +247,28 @@
         sends.append(copy)
         live_waits.append(send(livebox, livefrom.at[frm], l_send.at[d], l_recv.at[d], to, rep))
 
-    def ship(d, carry):
-        to = lax.rem(me + d, n_graph)
-        build(to)
-        send(outgoing.at[to], arrived.at[me], x_send.at[d], x_recv.at[d], to, rep).start()
-        return carry
-
-    lax.fori_loop(1, n_graph, ship, 0)
     key_waits = []
-    for d in range(1, n_graph):
-        to = lax.rem(me + d, n_graph)
-        frm = lax.rem(me + n_graph - d, n_graph)
-        sends.append(send(outgoing.at[to], arrived.at[me], x_send.at[d], x_recv.at[d], to, rep))
-        key_waits.append(send(outgoing.at[to], arrived.at[frm], x_send.at[d], x_recv.at[d], to, rep))
-    build(me)
-    arrived[me] = outgoing[me]
+    for h in range(2):
+
+        def ship(i, carry):
+            d = lax.rem(i, n_graph - 1) + 1
+            to = lax.rem(me + d, n_graph)
+            build(to, h)
+            send(outgoing.at[to, h], arrived[h].at[me], x_send.at[h * n_graph + d],
+                 x_recv.at[h * n_graph + d], to, rep).start()
+            return carry
+
+        lax.fori_loop(1, n_graph, ship, 0)
+        waits = []
+        for d in range(1, n_graph):
+            to = lax.rem(me + d, n_graph)
+            frm = lax.rem(me + n_graph - d, n_graph)
+            s_sem, r_sem = x_send.at[h * n_graph + d], x_recv.at[h * n_graph + d]
+            sends.append(send(outgoing.at[to, h], arrived[h].at[me], s_sem, r_sem, to, rep))
+            waits.append(send(outgoing.at[to, h], arrived[h].at[frm], s_sem, r_sem, to, rep))
+        key_waits.append(waits)
+        build(me, h)
+        arrived[h][me] = outgoing[me, h]
 
     def share(i, src, dst):
         copy = send(src, dst, sib_send.at[i], sib_recv.at[i], sibling, rep)
@@ -270,6 +279,8 @@
     share_nodes = share(0, nodes, nodes_s)
 
     rows = nodes[...].reshape(R, H)
+    loads[4].wait()
+    loads[5].wait()
     row_ids = lax.broadcasted_iota(jnp.int32, (R, E), 0)
     hot = jnp.concatenate(
         [
@@ -278,8 +289,9 @@
         ],
         axis=0,
     )
-    loads[0].wait()
-    loads[1].wait()
+    hot_t = hot.T
+    loads[6].wait()
+    loads[7].wait()
     pre = jnp.concatenate(
         [
             (dot_nn(rows, we1[:H]) + be[...]).astype(BF16),
@@ -287,115 +299,136 @@
         ],
         axis=0,
     )
-    summed = dot_tn(hot, pre)
+    summed = dot_nn(hot_t, pre)
     edge_sig = sigmoid(summed)
     gathered = dot_nn(hot[:R], (summed * edge_sig).astype(BF16)).astype(BF16)
     gat_f[...] = gathered
     share_gat = share(1, gat_f, gat_s)
-    loads[2].wait()
+    loads[8].wait()
     message = dot_nn(gathered, we2[...]).astype(BF16)
     msg_f[...] = message
     share_msg = share(2, msg_f, msg_s)
-    loads[3].wait()
-    loads[4].wait()
-    hidden_pre = dot_nn(rows, wn1[:H]) + dot_nn(message, wn1[H : 2 * H]) + bn[...]
+    loads[9].wait()
+    loads[10].wait()
+    hidden_part = dot_nn(rows, wn1[:H]) + dot_nn(message, wn1[H : 2 * H]) + bn[...]
     position = lax.broadcasted_iota(jnp.int32, (B, H), 0)
     mask = jnp.concatenate(
         [jnp.where(position < live[0, g], 1.0, 0.0) for g in range(G)], axis=0
     ) > 0.5
-    loads[5].wait()
-    loads[6].wait()
+    loads[11].wait()
+    loads[12].wait()
     grad_out = jnp.where(mask, cot[...].reshape(R, H).astype(F32), 0.0).astype(BF16)
     for c in range(2):
         go_f[c] = grad_out[:, c * (H // 2) : (c + 1) * (H // 2)]
     share_go = share(3, go_f.at[other], go_s)
     back_hidden = dot_nt(grad_out, wn2[...])
 
-    for copy in live_waits + key_waits:
+    def two_cores(mine, theirs):
+        return jnp.concatenate([mine, theirs], axis=0)
+
+    for copy in (share_nodes, share_gat, share_msg, share_go):
         copy.wait_recv()
+    nodes_t[...] = two_cores(rows, nodes_s[...].reshape(R, H)).T
+    msg_t[...] = two_cores(message, msg_s[...]).T
+    gat_t[...] = two_cores(gathered, gat_s[...]).T
+
     scale = H ** (-0.5)
+    lane = lax.broadcasted_iota(jnp.int32, (1, LANES), 1).astype(F32)
 
     def keys_of(g):
-        off = GMAX * B if g < half else 0
-        return arrived[owner[g], off : off + GMAX * B, :]
+        return arrived[1 if g < half else 0][owner[g]]
 
     def block(values, g):
         return values[g * B : (g + 1) * B]
 
-    lane = lax.broadcasted_iota(jnp.int32, (1, LANES), 1).astype(F32)
-    score_list, bound_list = [], []
-    for g in range(G):
-        score_list.append(dot_nt(block(rows, g), keys_of(g)))
+    def bound_of(g):
         at = partner[0, g] - owner[g] * G
         one = livefrom[owner[g], pl.ds(at, 1), :]
         two = livefrom[owner[g], pl.ds(jnp.minimum(at + 1, G - 1), 1), :]
         two = two * jnp.where(psize[0, g] > 1, 1.0, 0.0)
         bound = jnp.where(lane < B, one, B + two) - lane
-        bound_list.append(jnp.broadcast_to(bound[:, : GMAX * B], (B, GMAX * B)))
-    scores = jnp.concatenate(score_list, axis=0) * scale
-    scores = jnp.where(jnp.concatenate(bound_list, axis=0) > 0.5, scores, -jnp.inf)
-    powers = jnp.exp(scores - jnp.max(scores, axis=-1, keepdims=True))
-    probs = powers / jnp.sum(powers, axis=-1, keepdims=True)
-    low = probs.astype(BF16)
-    context = jnp.concatenate([dot_nn(block(low, g), keys_of(g)) for g in range(G)], axis=0)
-    moved = (rows.astype(F32) - context).astype(BF16)
-    moved_f[...] = moved
+        return jnp.broadcast_to(bound[:, : GMAX * B], (B, GMAX * B))
+
+    def attend(p):
+        part = range(p * half, (p + 1) * half)
+        at, to = p * half * B, (p + 1) * half * B
+        scores = jnp.concatenate([dot_nt(block(rows, g), keys_of(g)) for g in part], axis=0) * scale
+        bounds = jnp.concatenate([bound_of(g) for g in part], axis=0)
+        scores = jnp.where(bounds > 0.5, scores, -jnp.inf)
+        powers = jnp.exp(scores - jnp.max(scores, axis=-1, keepdims=True))
+        probs = powers / jnp.sum(powers, axis=-1, keepdims=True)
+        low = probs.astype(BF16)
+        context = jnp.concatenate(
+            [dot_nn(low[i * B : (i + 1) * B], keys_of(g)) for i, g in enumerate(part)], axis=0
+        )
+        moved = (rows[at:to].astype(F32) - context).astype(BF16)
+        moved_f[at:to, :] = moved
+        hidden_pre = hidden_part[at:to] + dot_nn(moved, wn1[2 * H :])
+        sig = sigmoid(hidden_pre)
+        grad_hidden = (back_hidden[at:to] * silu_slope(hidden_pre, sig)).astype(BF16)
+        for c in range(2):
+            gh_f[c, at:to, :] = grad_hidden[:, c * (FM // 2) : (c + 1) * (FM // 2)]
+        active = (hidden_pre * sig).astype(BF16)
+        act_f[at:to, :] = active
+        return probs, low, moved, grad_hidden, active
+
+    def message_back(p, grad_hidden):
+        at, to = p * half * B, (p + 1) * half * B
+        grad_message = dot_nt(grad_hidden, wn1[H : 2 * H]).astype(BF16)
+        for c in range(2):
+            gm_f[c, at:to, :] = grad_message[:, c * (H // 2) : (c + 1) * (H // 2)]
+        return dot_nt(grad_message, we2[...]).astype(BF16)
+
+    for copy in live_waits + key_waits[0]:
+        copy.wait_recv()
+    upper = attend(1)
+    upper_gathered = message_back(1, upper[3])
+    for copy in key_waits[1]:
+        copy.wait_recv()
+    lower = attend(0)
     share_moved = share(4, moved_f, moved_s)
-
-    hidden_pre = hidden_pre + dot_nn(moved, wn1[2 * H :])
-    sig = sigmoid(hidden_pre)
-    grad_hidden = (back_hidden * silu_slope(hidden_pre, sig)).astype(BF16)
-    for c in range(2):
-        gh_f[c] = grad_hidden[:, c * (FM // 2) : (c + 1) * (FM // 2)]
     share_gh = share(5, gh_f.at[other], gh_s)
-    active = (hidden_pre * sig).astype(BF16)
-    act_f[...] = active
     share_act = share(6, act_f, act_s)
-
-    grad_message = dot_nt(grad_hidden, wn1[H : 2 * H]).astype(BF16)
-    for c in range(2):
-        gm_f[c] = grad_message[:, c * (H // 2) : (c + 1) * (H // 2)]
+    lower_gathered = message_back(0, lower[3])
     share_gm = share(7, gm_f.at[other], gm_s)
-    grad_gathered = dot_nt(grad_message, we2[...]).astype(BF16)
-    edge_grad = (dot_tn(hot[:R], grad_gathered) * silu_slope(summed, edge_sig)).astype(BF16)
+    probs, low, moved, grad_hidden, active = (
+        jnp.concatenate([a, b], axis=0) for a, b in zip(lower, upper)
+    )
+    grad_gathered = jnp.concatenate([lower_gathered, upper_gathered], axis=0)
+    edge_grad = (dot_nn(hot_t[:, :R], grad_gathered) * silu_slope(summed, edge_sig)).astype(BF16)
     both = dot_nn(hot, edge_grad).astype(BF16)
     for c in range(2):
         gts_f[c] = both[:, c * (FM // 2) : (c + 1) * (FM // 2)]
     share_gts = share(8, gts_f.at[other], gts_s)
     grad_target, grad_source = both[:R], both[R:]
 
-    def two_cores(mine, theirs):
-        return jnp.concatenate([mine, theirs], axis=0)
-
-    for copy in (share_nodes, share_msg, share_moved, share_gh):
+    for copy in (share_moved, share_gh):
         copy.wait_recv()
-    rows2 = two_cores(rows, nodes_s[...].reshape(R, H))
     gh2 = two_cores(gh_f[core], gh_s[...])
     pieces = jnp.concatenate(
-        [dot_tn(rows2, gh2), dot_tn(two_cores(message, msg_s[...]), gh2),
+        [dot_nn(nodes_t[...], gh2), dot_nn(msg_t[...], gh2),
          dot_tn(two_cores(moved, moved_s[...]), gh2)],
         axis=0,
     )
     put_grad(ga.full, 0, pieces, n_rep)
     ga.first_plane()
 
-    for copy in (share_go, share_act):
-        copy.wait_recv()
+    share_act.wait_recv()
     piece = dot_tn(two_cores(active, act_s[...]), two_cores(go_f[core], go_s[...]))
     put_grad(gc.full, 0, piece, n_rep)
     cut = piece.shape[0] // n_rep * (piece.shape[1] // LANES)
     gc.first_rep(0, 0, cut)
 
-    for copy in (share_gat, share_gm):
-        copy.wait_recv()
-    piece = dot_tn(two_cores(gathered, gat_s[...]), two_cores(gm_f[core], gm_s[...]))
+    share_gm.wait_recv()
+    piece = dot_nn(gat_t[...], two_cores(gm_f[core], gm_s[...]))
     put_grad(gc.full, cut, piece, n_rep)
     gc.first_rep(1, cut, gc.full.shape[1])
 
     share_gts.wait_recv()
     mine, theirs = gts_f[core], gts_s[...]
     pieces = jnp.concatenate(
-        [dot_tn(rows2, two_cores(mine[:R], theirs[:R])), dot_tn(rows2, two_cores(mine[R:], theirs[R:]))],
+        [dot_nn(nodes_t[...], two_cores(mine[:R], theirs[:R])),
+         dot_nn(nodes_t[...], two_cores(mine[R:], theirs[R:]))],
         axis=0,
     )
     put_grad(gb.full, 0, pieces, n_rep)
@@ -445,15 +478,21 @@
 
     lax.fori_loop(0, n_graph, ship_back, 0)
     back[me] = backsend[me]
-    back_waits = []
-    for d in range(1, n_graph):
-        to = lax.rem(me + d, n_graph)
-        frm = lax.rem(me + n_graph - d, n_graph)
-        copy = send(backsend.at[to], back.at[me], b_send.at[d], b_recv.at[d], to, rep)
-        copy.start()
-        sends.append(copy)
-        back_waits.append(send(backsend.at[to], back.at[frm], b_send.at[d], b_recv.at[d], to, rep))
-
+
+    def start_back(h):
+        waits = []
+        for d in range(1, n_graph):
+            to = lax.rem(me + d, n_graph)
+            frm = lax.rem(me + n_graph - d, n_graph)
+            part = pl.ds(h * GMAX, GMAX)
+            s_sem, r_sem = b_send.at[h * n_graph + d], b_recv.at[h * n_graph + d]
+            copy = send(backsend.at[to, part], back.at[me, part], s_sem, r_sem, to, rep)
+            copy.start()
+            sends.append(copy)
+            waits.append(send(backsend.at[to, part], back.at[frm, part], s_sem, r_sem, to, rep))
+        return waits
+
+    back_waits = start_back(0)
     updated = jnp.where(mask, rows.astype(F32) + dot_nn(active, wn2[...]), 0.0)
     updated_out[...] = updated.astype(BF16).reshape(G, B, H)
     total = grad_out.astype(F32) + grad_moved.astype(F32)
@@ -480,7 +519,11 @@
         sends.append(copy)
         bias_waits.append(send(bias_m, bias_r.at[frm], d_send.at[d], d_recv.at[d], me, to))
     gc.second()
+    back_waits += start_back(1)
     gb.second()
+    ga.gather()
+    gc.gather()
+    gb.gather()
     for copy in back_waits:
         copy.wait_recv()
     returned = []
@@ -499,17 +542,14 @@
             row = row + bias_r[z, pl.ds(i * n_rep + rep, 1), :]
         bias_out[i : i + 1, :] = row
 
-    ga.gather()
-    gb.gather()
-    gc.gather()
-    ga.swap()
-    gb.swap()
-    gc.swap()
-    ga.finish(flat_a)
-    gb.finish(flat_b)
-    gc.finish(flat_c)
     for copy in sends:
         copy.wait_send()
+    ga.swap()
+    gc.swap()
+    gb.swap()
+    ga.finish(flat_a)
+    gc.finish(flat_c)
+    gb.finish(flat_b)
     for group in (ga, gb, gc):
         group.drain()
 
@@ -517,15 +557,31 @@
 def unpack(
     grad_scale, updated, dnodes, flat_a, flat_b, flat_c, bias,
     updated_out, dnodes_out, oe1, obe, oe2, on1, obn, on2,
+    ve1, vbe, ve2, vn1, vbn, vn2, sem,
 ):
-    updated_out[...] = updated[...]
-    dnodes_out[...] = dnodes[...]
-    take_grad(flat_a, 0, on1, grad_scale)
-    take_grad(flat_b, 0, oe1, grad_scale)
-    take_grad(flat_c, 0, on2, grad_scale)
-    take_grad(flat_c, on2.shape[0] * (on2.shape[1] // 2 // LANES), oe2, grad_scale)
-    obn[...] = bias[0:1, : obn.shape[1]] * grad_scale
-    obe[...] = bias[1:2, : obe.shape[1]] * grad_scale
+    copies = []
+
+    def put(src, dst):
+        copy = pltpu.make_async_copy(src, dst, sem.at[len(copies)])
+        copy.start()
+        copies.append(copy)
+
+    put(updated, updated_out)
+    put(dnodes, dnodes_out)
+    take_grad(flat_a, 0, vn1, grad_scale)
+    put(vn1, on1)
+    take_grad(flat_b, 0, ve1, grad_scale)
+    put(ve1, oe1)
+    take_grad(flat_c, 0, vn2, grad_scale)
+    put(vn2, on2)
+    take_grad(flat_c, on2.shape[0] * (on2.shape[1] // 2 // LANES), ve2, grad_scale)
+    put(ve2, oe2)
+    vbn[...] = bias[0:1, : vbn.shape[1]] * grad_scale
+    put(vbn, obn)
+    vbe[...] = bias[1:2, : vbe.shape[1]] * grad_scale
+    put(vbe, obe)
+    for copy in copies:
+        copy.wait()
 
 
 def group_scratch(shapes, n_graph, n_rep, plane_first):
@@ -556,8 +612,7 @@
     R = G * B
     dma = pltpu.SemaphoreType.DMA
     vmem = pl.BlockSpec(memory_space=pltpu.VMEM)
-    smem = pl.BlockSpec(memory_space=pltpu.SMEM)
-    hbm = pl.BlockSpec(memory_space=pl.ANY)
+    hbm = pl.BlockSpec(memory_space=pltpu.HBM)
     sds = jax.ShapeDtypeStruct
 
     def share(shape):
@@ -569,7 +624,9 @@
         group_scratch([w_node2.shape, w_edge2.shape], n_graph, n_rep, False),
     ]
     flats = tuple(sds((2 * g[0].shape[1], LANES), BF16) for g in groups)
-    weights = [cotangent[0], w_edge1, b_edge.reshape(1, FM), w_edge2, w_node1, b_node.reshape(1, FM), w_node2]
+    ints = [live, partner_first, partner_size]
+    arrays = [nodes[0], edge_src, edge_dst, w_edge1, b_edge.reshape(1, FM), w_edge2, w_node1,
+              b_node.reshape(1, FM), cotangent[0], w_node2]
 
     def wide(*shape):
         return pltpu.VMEM(shape, F32)
@@ -577,15 +634,13 @@
     def bf(*shape):
         return pltpu.VMEM(shape, BF16)
 
-    parts = pl.pallas_call(
-        functools.partial(kernel, n_graph, n_rep),
-        out_shape=(sds((G, B, H), BF16), sds((G, B, H), BF16)) + flats + (sds((2, LANES), F32),),
-        in_specs=[vmem, smem, smem, smem, vmem, vmem] + [hbm] * 7,
-        out_specs=(vmem,) * 6,
-        scratch_shapes=[pltpu.VMEM(w.shape, w.dtype) for w in weights]
+    scratch = (
+        [pltpu.SMEM(w.shape, w.dtype) for w in ints]
+        + [pltpu.VMEM(w.shape, w.dtype) for w in arrays]
         + [
-            bf(n_graph, 2 * GMAX * B, H),
-            bf(n_graph, 2 * GMAX * B, H),
+            bf(n_graph, 2, GMAX * B, H),
+            bf(n_graph, GMAX * B, H),
+            bf(n_graph, GMAX * B, H),
             wide(G, LANES),
             wide(n_graph, G, LANES),
             wide(G, GMAX * B, H),
@@ -596,32 +651,42 @@
             bf(2, R, H // 2), bf(2, 2 * R, FM // 2),
             bf(G, B, H), bf(R, H), bf(R, H), bf(R, FM // 2), bf(R, FM), bf(R, H // 2), bf(R, FM),
             bf(R, H // 2), bf(2 * R, FM // 2),
+            bf(H, 2 * R), bf(H, 2 * R), bf(FM, 2 * R),
             wide(2 * n_rep, LANES), wide(n_graph, 2 * n_rep, LANES), wide(2 * n_rep, LANES),
             wide(n_rep, 2 * n_rep, LANES),
-            dma((7,)),
-            dma((n_graph,)), dma((n_graph,)), dma((n_graph,)), dma((n_graph,)),
-            dma((n_graph,)), dma((n_graph,)), dma((9,)), dma((9,)),
+            dma((13,)),
+            dma((2 * n_graph,)), dma((2 * n_graph,)), dma((n_graph,)), dma((n_graph,)),
+            dma((2 * n_graph,)), dma((2 * n_graph,)), dma((9,)), dma((9,)),
             dma((n_graph,)), dma((n_graph,)), dma((n_rep,)), dma((n_rep,)),
         ]
-        + sum(groups, []),
+        + sum(groups, [])
+    )
+    held = sum(math.prod(w.shape) * w.dtype.itemsize for w in scratch if w.dtype in (BF16, F32))
+    parts = pl.pallas_call(
+        functools.partial(kernel, n_graph, n_rep),
+        out_shape=(sds((G, B, H), BF16), sds((G, B, H), BF16)) + flats + (sds((2, LANES), F32),),
+        in_specs=[hbm] * 13,
+        out_specs=(vmem,) * 6,
+        scratch_shapes=scratch,
         compiler_params=pltpu.CompilerParams(
-            collective_id=0, has_side_effects=True, vmem_limit_bytes=64 * 1000 * 1000
+            collective_id=0, has_side_effects=True, vmem_limit_bytes=min(2 * held, 64 * 1000 * 1000)
         ),
-    )(nodes[0], live, partner_first, partner_size, edge_src, edge_dst, *weights)
+    )(*[pltpu.with_memory_space_constraint(a, pltpu.HBM) for a in ints + arrays])
+    shapes = (
+        share(w_edge1.shape),
+        sds((1, FM // n_rep), F32),
+        share(w_edge2.shape),
+        share(w_node1.shape),
+        sds((1, FM // n_rep), F32),
+        share(w_node2.shape),
+    )
     outs = pl.pallas_call(
         functools.partial(unpack, (n_graph * n_rep * G * B) ** (-0.5)),
-        out_shape=(
-            sds((G, B, H), BF16),
-            sds((G, B, H), BF16),
-            share(w_edge1.shape),
-            sds((1, FM // n_rep), F32),
-            share(w_edge2.shape),
-            share(w_node1.shape),
-            sds((1, FM // n_rep), F32),
-            share(w_node2.shape),
-        ),
+        out_shape=(sds((G, B, H), BF16), sds((G, B, H), BF16)) + shapes,
         in_specs=[vmem] * 6,
-        out_specs=(vmem,) * 8,
+        out_specs=(hbm,) * 8,
+        scratch_shapes=[pltpu.VMEM(w.shape, F32) for w in shapes] + [dma((8,))],
+        compiler_params=pltpu.CompilerParams(vmem_limit_bytes=16 * 1000 * 1000),
     )(*parts)
     return (
         outs[0][None],

time: 42.9 us -> 39 us (0.909)
  Pallas kernels: 42.1 us -> 38.2 us
    pallas_call x1, Pallas kernels: 39.8 us -> 37.1 us  [on_device(): pl.pallas_call(functools.partial(kernel, n_graph, n_rep), out_shape=(sds(...]
    pallas_call x1, Pallas kernels: 2.23 us -> 1.08 us  [on_device(): pl.pallas_call(functools.partial(unpack, (n_graph * n_rep * G * B) ** (-0...]
where the time goes in v2:
time: 39 us; the launch traced here: 38.8 us
  Pallas kernels  38.2 us (98%)
  between operations  0.65 us (2%)
    pallas_call x1, Pallas kernels, on_device(): pl.pallas_call(functools.partial(kernel, n_graph, n_rep), out_shape=(sds(...  37.1 us
    pallas_call x1, Pallas kernels, on_device(): pl.pallas_call(functools.partial(unpack, (n_graph * n_rep * G * B) ** (-0...  1.08 us

profile of v2, /device:TPU:0, one launch (start us, length us, event | category | flops | bytes accessed | tf_op | source)
XLA Modules:
  0.0 38.8 jit_solution(220926099345658802)
XLA Ops:
  0.6 37.1 %shard_map.188 = (bf16[8,32,256]{2,1,0:T(8,128)(2,1)S(1)}, bf16[8,32,256]{2,1,0:T(8,128)(2,1)S(1)}, bf16[768,128]{1,0:T(8,128)(2,1)S(1)}, bf16[512,128]{1,0:T(8,...) custom-call(s32[1,8]{1,0:T(1,128)} %refs_0_.1, s32[1,8]{1,0:T(1,128)} %refs_1_.1, s32[1,8]{1,0:T(1,128)} %refs_2_.1, ...), custom_call_target="tpu_custom_call" | custom-call | tf_op jit(solution)/shard_map/pallas_call | solution.py:665
  37.7 1.1 %shard_map.189 = (bf16[8,32,256]{2,1,0:T(8,128)(2,1)}, bf16[8,32,256]{2,1,0:T(8,128)(2,1)}, f32[128,512]{1,0:T(8,128)}, f32[1,128]{1,0:T(1,128)}, f32[128,256]{1...) custom-call(bf16[8,32,256]{2,1,0:T(8,128)(2,1)S(1)} %get-tuple-element.22.updated, ...), custom_call_target="tpu_custom_call" | custom-call | tf_op jit(solution)/shard_map/pallas_call | solution.py:683

commit v3 on v2

--- a/solution.py
+++ b/solution.py
@@ -9,6 +9,7 @@
 from jax.sharding import PartitionSpec as P
 
 GMAX = 2
+MARK = 64.0
 LANES = 128
 F32 = jnp.float32
 BF16 = jnp.bfloat16
@@ -109,7 +110,7 @@
         else:
             self.seconds = self.over_plane(lambda q: self.b.at[self.rows(q)], self.r2, self.s2, self.v2)
 
-    def gather(self):
+    def gather(self, direct=False):
         if self.plane_first:
             total = self.b[self.rep].astype(F32)
             count = self.r
@@ -123,6 +124,15 @@
         place = self.core * self.chips + self.chip
         self.got[place] = total.astype(BF16)
         self.thirds = []
+        if direct:
+            for d in range(1, self.n):
+                to = lax.rem(self.me + d, self.n)
+                frm = lax.rem(self.me + self.n - d, self.n)
+                theirs = lax.rem(frm, 2) * self.chips + lax.div(frm, 2)
+                self.go(send(self.got.at[place], self.got.at[place], self.s3.at[d], self.v3.at[d], to, self.rep))
+                self.thirds.append(send(self.got.at[theirs], self.got.at[theirs], self.s3.at[d], self.v3.at[d],
+                                        to, self.rep))
+            return
         for d in range(1, self.chips):
             to = lax.rem(self.chip + d, self.chips) * 2 + self.core
             frm = self.core * self.chips + lax.rem(self.chip + self.chips - d, self.chips)
@@ -140,13 +150,15 @@
         self.go(send(mine, mine, self.s3.at[0], self.v3.at[0], to, self.rep))
         self.last = send(theirs, theirs, self.s3.at[0], self.v3.at[0], to, self.rep)
 
-    def finish(self, out):
-        self.last.wait_recv()
+    def finish(self, out, direct=False):
+        for copy in self.thirds if direct else [self.last]:
+            copy.wait_recv()
         out[...] = self.got[...].reshape(self.n * self.ch, LANES)
 
     def drain(self):
         for copy in self.sends:
             copy.wait_send()
+        self.sends = []
 
 
 def put_grad(full, offset, grad, n_rep):
@@ -177,17 +189,17 @@
     n_graph, n_rep,
     *refs
 ):
-    ins, outs, held, rest = refs[:13], refs[13:19], refs[19:32], refs[32:]
-    live, partner, psize, nodes, src_ref, dst_ref, we1, be, we2, wn1, bn, cot, wn2 = held
+    ins, outs, held, rest = refs[:12], refs[12:18], refs[18:30], refs[30:]
+    live, partner, nodes, src_ref, dst_ref, we1, be, we2, wn1, bn, cot, wn2 = held
     updated_out, dnodes_out, flat_a, flat_b, flat_c, bias_out = outs
-    (outgoing, arrived_low, arrived_high, livebox, livefrom, keygrad, backsend, back, inv,
+    (outgoing, arrived_low, arrived_high, keygrad, backsend, back, inv,
      msg_f, moved_f, gh_f, act_f, go_f, gat_f, gm_f, gts_f,
      nodes_s, msg_s, moved_s, gh_s, act_s, go_s, gat_s, gm_s, gts_s,
      nodes_t, msg_t, gat_t,
      bias_f, bias_g, bias_m, bias_r,
-     load_sem, x_send, x_recv, l_send, l_recv, b_send, b_recv, sib_send, sib_recv,
-     c_send, c_recv, d_send, d_recv) = rest[:46]
-    group_refs = rest[46:]
+     load_sem, x_send, x_recv, b_send, b_recv, sib_send, sib_recv,
+     c_send, c_recv, d_send, d_recv) = rest[:42]
+    group_refs = rest[42:]
     arrived = (arrived_low, arrived_high)
     me = lax.axis_index("graph")
     rep = lax.axis_index("rep")
@@ -216,12 +228,15 @@
     for d in range(1, n_rep):
         pl.semaphore_signal(barrier, inc=1, device_id={"graph": me, "rep": lax.rem(rep + d, n_rep)},
                             device_id_type=pl.DeviceIdType.MESH)
-    for copy in loads[:4]:
+    for copy in loads[:3]:
         copy.wait()
     owner = [lax.div(partner[0, g], G) for g in range(G)]
-    for g in range(G):
-        livebox[g : g + 1, :] = jnp.full((1, LANES), live[0, g].astype(F32))
-    livefrom[me] = livebox[...]
+    mark_row = lax.broadcasted_iota(jnp.int32, (B, LANES), 0)
+    mark_lane = lax.broadcasted_iota(jnp.int32, (B, LANES), 1)
+
+    def marked(g, count):
+        mark = jnp.where(mark_row >= count, jnp.where(mark_lane == 0, MARK, 0.0), 0.0)
+        return (nodes[g, :, :LANES].astype(F32) + mark).astype(BF16)
 
     def build(p, h):
         first = jnp.int32(0)
@@ -232,21 +247,15 @@
             count = count + jnp.where(hit, 1, 0)
         inv[0, p * 2 + h] = first
         inv[1, p * 2 + h] = count
-        outgoing[p, h, :B, :] = nodes[first]
-        outgoing[p, h, B:, :] = nodes[jnp.minimum(first + 1, G - 1)]
+        second = jnp.minimum(first + 1, G - 1)
+        outgoing[p, h, :B, :LANES] = marked(first, live[0, first])
+        outgoing[p, h, B:, :LANES] = marked(second, jnp.where(count > 1, live[0, second], 0))
+        outgoing[p, h, :B, LANES:] = nodes[first, :, LANES:]
+        outgoing[p, h, B:, LANES:] = nodes[second, :, LANES:]
 
     pl.semaphore_wait(barrier, n_graph + n_rep - 2)
 
     sends = []
-    live_waits = []
-    for d in range(1, n_graph):
-        to = lax.rem(me + d, n_graph)
-        frm = lax.rem(me + n_graph - d, n_graph)
-        copy = send(livebox, livefrom.at[me], l_send.at[d], l_recv.at[d], to, rep)
-        copy.start()
-        sends.append(copy)
-        live_waits.append(send(livebox, livefrom.at[frm], l_send.at[d], l_recv.at[d], to, rep))
-
     key_waits = []
     for h in range(2):
 
@@ -279,8 +288,8 @@
     share_nodes = share(0, nodes, nodes_s)
 
     rows = nodes[...].reshape(R, H)
+    loads[3].wait()
     loads[4].wait()
-    loads[5].wait()
     row_ids = lax.broadcasted_iota(jnp.int32, (R, E), 0)
     hot = jnp.concatenate(
         [
@@ -290,8 +299,8 @@
         axis=0,
     )
     hot_t = hot.T
+    loads[5].wait()
     loads[6].wait()
-    loads[7].wait()
     pre = jnp.concatenate(
         [
             (dot_nn(rows, we1[:H]) + be[...]).astype(BF16),
@@ -304,19 +313,19 @@
     gathered = dot_nn(hot[:R], (summed * edge_sig).astype(BF16)).astype(BF16)
     gat_f[...] = gathered
     share_gat = share(1, gat_f, gat_s)
-    loads[8].wait()
+    loads[7].wait()
     message = dot_nn(gathered, we2[...]).astype(BF16)
     msg_f[...] = message
     share_msg = share(2, msg_f, msg_s)
+    loads[8].wait()
     loads[9].wait()
-    loads[10].wait()
     hidden_part = dot_nn(rows, wn1[:H]) + dot_nn(message, wn1[H : 2 * H]) + bn[...]
     position = lax.broadcasted_iota(jnp.int32, (B, H), 0)
     mask = jnp.concatenate(
         [jnp.where(position < live[0, g], 1.0, 0.0) for g in range(G)], axis=0
     ) > 0.5
+    loads[10].wait()
     loads[11].wait()
-    loads[12].wait()
     grad_out = jnp.where(mask, cot[...].reshape(R, H).astype(F32), 0.0).astype(BF16)
     for c in range(2):
         go_f[c] = grad_out[:, c * (H // 2) : (c + 1) * (H // 2)]
@@ -333,28 +342,22 @@
     gat_t[...] = two_cores(gathered, gat_s[...]).T
 
     scale = H ** (-0.5)
-    lane = lax.broadcasted_iota(jnp.int32, (1, LANES), 1).astype(F32)
+    first_lane = lax.broadcasted_iota(jnp.int32, (16, H), 1) == 0
+    pick = jnp.where(first_lane, 1.0, 0.0).astype(BF16)
 
     def keys_of(g):
         return arrived[1 if g < half else 0][owner[g]]
 
     def block(values, g):
         return values[g * B : (g + 1) * B]
-
-    def bound_of(g):
-        at = partner[0, g] - owner[g] * G
-        one = livefrom[owner[g], pl.ds(at, 1), :]
-        two = livefrom[owner[g], pl.ds(jnp.minimum(at + 1, G - 1), 1), :]
-        two = two * jnp.where(psize[0, g] > 1, 1.0, 0.0)
-        bound = jnp.where(lane < B, one, B + two) - lane
-        return jnp.broadcast_to(bound[:, : GMAX * B], (B, GMAX * B))
 
     def attend(p):
         part = range(p * half, (p + 1) * half)
         at, to = p * half * B, (p + 1) * half * B
-        scores = jnp.concatenate([dot_nt(block(rows, g), keys_of(g)) for g in part], axis=0) * scale
-        bounds = jnp.concatenate([bound_of(g) for g in part], axis=0)
-        scores = jnp.where(bounds > 0.5, scores, -jnp.inf)
+        products = [dot_nt(jnp.concatenate([block(rows, g), pick], axis=0), keys_of(g)) for g in part]
+        marks = jnp.concatenate([jnp.broadcast_to(v[B : B + 1], (B, GMAX * B)) for v in products], axis=0)
+        scores = jnp.concatenate([v[:B] for v in products], axis=0) * scale
+        scores = jnp.where(marks < 0.5 * MARK, scores, -jnp.inf)
         powers = jnp.exp(scores - jnp.max(scores, axis=-1, keepdims=True))
         probs = powers / jnp.sum(powers, axis=-1, keepdims=True)
         low = probs.astype(BF16)
@@ -368,9 +371,12 @@
         grad_hidden = (back_hidden[at:to] * silu_slope(hidden_pre, sig)).astype(BF16)
         for c in range(2):
             gh_f[c, at:to, :] = grad_hidden[:, c * (FM // 2) : (c + 1) * (FM // 2)]
+        return probs, low, moved, grad_hidden, hidden_pre, sig
+
+    def activate(p, hidden_pre, sig):
         active = (hidden_pre * sig).astype(BF16)
-        act_f[at:to, :] = active
-        return probs, low, moved, grad_hidden, active
+        act_f[p * half * B : (p + 1) * half * B, :] = active
+        return active
 
     def message_back(p, grad_hidden):
         at, to = p * half * B, (p + 1) * half * B
@@ -379,21 +385,42 @@
             gm_f[c, at:to, :] = grad_message[:, c * (H // 2) : (c + 1) * (H // 2)]
         return dot_nt(grad_message, we2[...]).astype(BF16)
 
-    for copy in live_waits + key_waits[0]:
+    for copy in key_waits[0]:
         copy.wait_recv()
     upper = attend(1)
+    upper_active = activate(1, *upper[4:])
     upper_gathered = message_back(1, upper[3])
     for copy in key_waits[1]:
         copy.wait_recv()
     lower = attend(0)
     share_moved = share(4, moved_f, moved_s)
     share_gh = share(5, gh_f.at[other], gh_s)
+    lower_active = activate(0, *lower[4:])
     share_act = share(6, act_f, act_s)
     lower_gathered = message_back(0, lower[3])
     share_gm = share(7, gm_f.at[other], gm_s)
-    probs, low, moved, grad_hidden, active = (
-        jnp.concatenate([a, b], axis=0) for a, b in zip(lower, upper)
-    )
+    probs, low, moved, grad_hidden = (
+        jnp.concatenate([a, b], axis=0) for a, b in zip(lower[:4], upper[:4])
+    )
+    active = jnp.concatenate([lower_active, upper_active], axis=0)
+
+    def node_pieces(part, moved_rows, gh):
+        return jnp.concatenate(
+            [dot_nn(nodes_t[:, part], gh), dot_nn(msg_t[:, part], gh), dot_tn(moved_rows, gh)], axis=0
+        )
+
+    mine = node_pieces(slice(0, R), moved, gh_f[core])
+    for copy in (share_moved, share_gh):
+        copy.wait_recv()
+    put_grad(ga.full, 0, mine + node_pieces(slice(R, 2 * R), moved_s[...], gh_s[...]), n_rep)
+    ga.first_plane()
+
+    share_act.wait_recv()
+    piece = dot_tn(two_cores(active, act_s[...]), two_cores(go_f[core], go_s[...]))
+    put_grad(gc.full, 0, piece, n_rep)
+    cut = piece.shape[0] // n_rep * (piece.shape[1] // LANES)
+    gc.first_rep(0, 0, cut)
+
     grad_gathered = jnp.concatenate([lower_gathered, upper_gathered], axis=0)
     edge_grad = (dot_nn(hot_t[:, :R], grad_gathered) * silu_slope(summed, edge_sig)).astype(BF16)
     both = dot_nn(hot, edge_grad).astype(BF16)
@@ -402,37 +429,10 @@
     share_gts = share(8, gts_f.at[other], gts_s)
     grad_target, grad_source = both[:R], both[R:]
 
-    for copy in (share_moved, share_gh):
-        copy.wait_recv()
-    gh2 = two_cores(gh_f[core], gh_s[...])
-    pieces = jnp.concatenate(
-        [dot_nn(nodes_t[...], gh2), dot_nn(msg_t[...], gh2),
-         dot_tn(two_cores(moved, moved_s[...]), gh2)],
-        axis=0,
-    )
-    put_grad(ga.full, 0, pieces, n_rep)
-    ga.first_plane()
-
-    share_act.wait_recv()
-    piece = dot_tn(two_cores(active, act_s[...]), two_cores(go_f[core], go_s[...]))
-    put_grad(gc.full, 0, piece, n_rep)
-    cut = piece.shape[0] // n_rep * (piece.shape[1] // LANES)
-    gc.first_rep(0, 0, cut)
-
     share_gm.wait_recv()
     piece = dot_nn(gat_t[...], two_cores(gm_f[core], gm_s[...]))
     put_grad(gc.full, cut, piece, n_rep)
     gc.first_rep(1, cut, gc.full.shape[1])
-
-    share_gts.wait_recv()
-    mine, theirs = gts_f[core], gts_s[...]
-    pieces = jnp.concatenate(
-        [dot_nn(nodes_t[...], two_cores(mine[:R], theirs[:R])),
-         dot_nn(nodes_t[...], two_cores(mine[R:], theirs[R:]))],
-        axis=0,
-    )
-    put_grad(gb.full, 0, pieces, n_rep)
-    gb.first_plane()
 
     width = FM // n_rep
     sums = (jnp.sum(grad_hidden.astype(F32), axis=0, keepdims=True),
@@ -452,6 +452,16 @@
         copy.start()
         sends.append(copy)
         bias_waits.append(send(bias_f, bias_g.at[frm], c_send.at[d], c_recv.at[d], to, rep))
+
+    share_gts.wait_recv()
+    mine, theirs = gts_f[core], gts_s[...]
+    pieces = jnp.concatenate(
+        [dot_nn(nodes_t[...], two_cores(mine[:R], theirs[:R])),
+         dot_nn(nodes_t[...], two_cores(mine[R:], theirs[R:]))],
+        axis=0,
+    )
+    put_grad(gb.full, 0, pieces, n_rep)
+    gb.first_plane()
 
     grad_moved = dot_nt(grad_hidden, wn1[2 * H :]).astype(BF16)
     negated = -grad_moved
@@ -521,9 +531,12 @@
     gc.second()
     back_waits += start_back(1)
     gb.second()
+    ga.drain()
     ga.gather()
+    gc.drain()
     gc.gather()
-    gb.gather()
+    gb.drain()
+    gb.gather(direct=True)
     for copy in back_waits:
         copy.wait_recv()
     returned = []
@@ -546,10 +559,9 @@
         copy.wait_send()
     ga.swap()
     gc.swap()
-    gb.swap()
     ga.finish(flat_a)
     gc.finish(flat_c)
-    gb.finish(flat_b)
+    gb.finish(flat_b, direct=True)
     for group in (ga, gb, gc):
         group.drain()
 
@@ -624,7 +636,7 @@
         group_scratch([w_node2.shape, w_edge2.shape], n_graph, n_rep, False),
     ]
     flats = tuple(sds((2 * g[0].shape[1], LANES), BF16) for g in groups)
-    ints = [live, partner_first, partner_size]
+    ints = [live, partner_first]
     arrays = [nodes[0], edge_src, edge_dst, w_edge1, b_edge.reshape(1, FM), w_edge2, w_node1,
               b_node.reshape(1, FM), cotangent[0], w_node2]
 
@@ -641,8 +653,6 @@
             bf(n_graph, 2, GMAX * B, H),
             bf(n_graph, GMAX * B, H),
             bf(n_graph, GMAX * B, H),
-            wide(G, LANES),
-            wide(n_graph, G, LANES),
             wide(G, GMAX * B, H),
             bf(n_graph, 2 * GMAX, B, H),
             bf(n_graph, 2 * GMAX, B, H),
@@ -654,8 +664,8 @@
             bf(H, 2 * R), bf(H, 2 * R), bf(FM, 2 * R),
             wide(2 * n_rep, LANES), wide(n_graph, 2 * n_rep, LANES), wide(2 * n_rep, LANES),
             wide(n_rep, 2 * n_rep, LANES),
-            dma((13,)),
-            dma((2 * n_graph,)), dma((2 * n_graph,)), dma((n_graph,)), dma((n_graph,)),
+            dma((12,)),
+            dma((2 * n_graph,)), dma((2 * n_graph,)),
             dma((2 * n_graph,)), dma((2 * n_graph,)), dma((9,)), dma((9,)),
             dma((n_graph,)), dma((n_graph,)), dma((n_rep,)), dma((n_rep,)),
         ]
@@ -665,7 +675,7 @@
     parts = pl.pallas_call(
         functools.partial(kernel, n_graph, n_rep),
         out_shape=(sds((G, B, H), BF16), sds((G, B, H), BF16)) + flats + (sds((2, LANES), F32),),
-        in_specs=[hbm] * 13,
+        in_specs=[hbm] * 12,
         out_specs=(vmem,) * 6,
         scratch_shapes=scratch,
         compiler_params=pltpu.CompilerParams(

time: 39 us -> 37.9 us (0.972)
  Pallas kernels: 38.2 us -> 37.1 us
    pallas_call x1, Pallas kernels: 37.1 us -> 36 us  [on_device(): pl.pallas_call(functools.partial(kernel, n_graph, n_rep), out_shape=(sds(...]
where the time goes in v3:
time: 37.9 us; the launch traced here: 37.7 us
  Pallas kernels  37.1 us (98%)
  between operations  0.65 us (2%)
    pallas_call x1, Pallas kernels, on_device(): pl.pallas_call(functools.partial(kernel, n_graph, n_rep), out_shape=(sds(...  36 us
    pallas_call x1, Pallas kernels, on_device(): pl.pallas_call(functools.partial(unpack, (n_graph * n_rep * G * B) ** (-0...  1.08 us

profile of v3, /device:TPU:0, one launch (start us, length us, event | category | flops | bytes accessed | tf_op | source)
XLA Modules:
  0.0 37.7 jit_solution(16324067340764946918)
XLA Ops:
  0.6 36.0 %shard_map.179 = (bf16[8,32,256]{2,1,0:T(8,128)(2,1)S(1)}, bf16[8,32,256]{2,1,0:T(8,128)(2,1)S(1)}, bf16[768,128]{1,0:T(8,128)(2,1)S(1)}, bf16[512,128]{1,0:T(8,...) custom-call(s32[1,8]{1,0:T(1,128)} %refs_0_.1, s32[1,8]{1,0:T(1,128)} %refs_1_.1, ...), custom_call_target="tpu_custom_call" | custom-call | tf_op jit(solution)/shard_map/pallas_call | solution.py:675
  36.7 1.1 %shard_map.180 = (bf16[8,32,256]{2,1,0:T(8,128)(2,1)}, bf16[8,32,256]{2,1,0:T(8,128)(2,1)}, f32[128,512]{1,0:T(8,128)}, f32[1,128]{1,0:T(1,128)}, f32[128,256]{1...) custom-call(bf16[8,32,256]{2,1,0:T(8,128)(2,1)S(1)} %get-tuple-element.22.updated, ...), custom_call_target="tpu_custom_call" | custom-call | tf_op jit(solution)/shard_map/pallas_call | solution.py:693

commit v4 on v3

--- a/solution.py
+++ b/solution.py
@@ -387,16 +387,24 @@
 
     for copy in key_waits[0]:
         copy.wait_recv()
+    def share_part(i, p, src, dst):
+        part = pl.ds(p * half * B, half * B)
+        return share(i, src.at[part], dst.at[part])
+
+    def share_moves(p):
+        return [share_part(9 + p, p, moved_f, moved_s), share_part(11 + p, p, gh_f.at[other], gh_s)]
+
     upper = attend(1)
+    share_mine = share_moves(1)
     upper_active = activate(1, *upper[4:])
+    share_act = [share_part(14, 1, act_f, act_s)]
     upper_gathered = message_back(1, upper[3])
     for copy in key_waits[1]:
         copy.wait_recv()
     lower = attend(0)
-    share_moved = share(4, moved_f, moved_s)
-    share_gh = share(5, gh_f.at[other], gh_s)
+    share_mine += share_moves(0)
     lower_active = activate(0, *lower[4:])
-    share_act = share(6, act_f, act_s)
+    share_act += [share_part(13, 0, act_f, act_s)]
     lower_gathered = message_back(0, lower[3])
     share_gm = share(7, gm_f.at[other], gm_s)
     probs, low, moved, grad_hidden = (
@@ -410,17 +418,7 @@
         )
 
     mine = node_pieces(slice(0, R), moved, gh_f[core])
-    for copy in (share_moved, share_gh):
-        copy.wait_recv()
-    put_grad(ga.full, 0, mine + node_pieces(slice(R, 2 * R), moved_s[...], gh_s[...]), n_rep)
-    ga.first_plane()
-
-    share_act.wait_recv()
-    piece = dot_tn(two_cores(active, act_s[...]), two_cores(go_f[core], go_s[...]))
-    put_grad(gc.full, 0, piece, n_rep)
-    cut = piece.shape[0] // n_rep * (piece.shape[1] // LANES)
-    gc.first_rep(0, 0, cut)
-
+    piece = dot_tn(active, go_f[core])
     grad_gathered = jnp.concatenate([lower_gathered, upper_gathered], axis=0)
     edge_grad = (dot_nn(hot_t[:, :R], grad_gathered) * silu_slope(summed, edge_sig)).astype(BF16)
     both = dot_nn(hot, edge_grad).astype(BF16)
@@ -428,6 +426,18 @@
         gts_f[c] = both[:, c * (FM // 2) : (c + 1) * (FM // 2)]
     share_gts = share(8, gts_f.at[other], gts_s)
     grad_target, grad_source = both[:R], both[R:]
+
+    for copy in share_mine:
+        copy.wait_recv()
+    put_grad(ga.full, 0, mine + node_pieces(slice(R, 2 * R), moved_s[...], gh_s[...]), n_rep)
+    ga.first_plane()
+
+    for copy in share_act:
+        copy.wait_recv()
+    piece = piece + dot_tn(act_s[...], go_s[...])
+    put_grad(gc.full, 0, piece, n_rep)
+    cut = piece.shape[0] // n_rep * (piece.shape[1] // LANES)
+    gc.first_rep(0, 0, cut)
 
     share_gm.wait_recv()
     piece = dot_nn(gat_t[...], two_cores(gm_f[core], gm_s[...]))
@@ -442,16 +452,16 @@
             row = sums[i][:, z * width : (z + 1) * width]
             if width < LANES:
                 row = jnp.concatenate([row, jnp.zeros((1, LANES - width), F32)], axis=1)
-            bias_f[i * n_rep + z : i * n_rep + z + 1, :] = row
-    bias_g[me] = bias_f[...]
+            bias_f[z, i : i + 1, :] = row
+    bias_r[rep] = bias_f[rep]
     bias_waits = []
-    for d in range(1, n_graph):
-        to = lax.rem(me + d, n_graph)
-        frm = lax.rem(me + n_graph - d, n_graph)
-        copy = send(bias_f, bias_g.at[me], c_send.at[d], c_recv.at[d], to, rep)
+    for d in range(1, n_rep):
+        to = lax.rem(rep + d, n_rep)
+        frm = lax.rem(rep + n_rep - d, n_rep)
+        copy = send(bias_f.at[to], bias_r.at[rep], d_send.at[d], d_recv.at[d], me, to)
         copy.start()
         sends.append(copy)
-        bias_waits.append(send(bias_f, bias_g.at[frm], c_send.at[d], c_recv.at[d], to, rep))
+        bias_waits.append(send(bias_f.at[to], bias_r.at[frm], d_send.at[d], d_recv.at[d], me, to))
 
     share_gts.wait_recv()
     mine, theirs = gts_f[core], gts_s[...]
@@ -515,19 +525,19 @@
     ga.second()
     for copy in bias_waits:
         copy.wait_recv()
-    summed_bias = bias_g[0]
-    for i in range(1, n_graph):
-        summed_bias = summed_bias + bias_g[i]
+    summed_bias = bias_r[0]
+    for z in range(1, n_rep):
+        summed_bias = summed_bias + bias_r[z]
     bias_m[...] = summed_bias
-    bias_r[rep] = summed_bias
+    bias_g[me] = summed_bias
     bias_waits = []
-    for d in range(1, n_rep):
-        to = lax.rem(rep + d, n_rep)
-        frm = lax.rem(rep + n_rep - d, n_rep)
-        copy = send(bias_m, bias_r.at[rep], d_send.at[d], d_recv.at[d], me, to)
+    for d in range(1, n_graph):
+        to = lax.rem(me + d, n_graph)
+        frm = lax.rem(me + n_graph - d, n_graph)
+        copy = send(bias_m, bias_g.at[me], c_send.at[d], c_recv.at[d], to, rep)
         copy.start()
         sends.append(copy)
-        bias_waits.append(send(bias_m, bias_r.at[frm], d_send.at[d], d_recv.at[d], me, to))
+        bias_waits.append(send(bias_m, bias_g.at[frm], c_send.at[d], c_recv.at[d], to, rep))
     gc.second()
     back_waits += start_back(1)
     gb.second()
@@ -537,6 +547,8 @@
     gc.gather()
     gb.drain()
     gb.gather(direct=True)
+    ga.swap()
+    gc.swap()
     for copy in back_waits:
         copy.wait_recv()
     returned = []
@@ -549,16 +561,12 @@
     dnodes_out[...] = jnp.where(mask, total, 0.0).astype(BF16).reshape(G, B, H)
     for copy in bias_waits:
         copy.wait_recv()
-    for i in range(2):
-        row = bias_r[0, pl.ds(i * n_rep + rep, 1), :]
-        for z in range(1, n_rep):
-            row = row + bias_r[z, pl.ds(i * n_rep + rep, 1), :]
-        bias_out[i : i + 1, :] = row
-
+    summed_bias = bias_g[0]
+    for i in range(1, n_graph):
+        summed_bias = summed_bias + bias_g[i]
+    bias_out[...] = summed_bias
     for copy in sends:
         copy.wait_send()
-    ga.swap()
-    gc.swap()
     ga.finish(flat_a)
     gc.finish(flat_c)
     gb.finish(flat_b, direct=True)
@@ -662,11 +670,10 @@
             bf(G, B, H), bf(R, H), bf(R, H), bf(R, FM // 2), bf(R, FM), bf(R, H // 2), bf(R, FM),
             bf(R, H // 2), bf(2 * R, FM // 2),
             bf(H, 2 * R), bf(H, 2 * R), bf(FM, 2 * R),
-            wide(2 * n_rep, LANES), wide(n_graph, 2 * n_rep, LANES), wide(2 * n_rep, LANES),
-            wide(n_rep, 2 * n_rep, LANES),
+            wide(n_rep, 2, LANES), wide(n_graph, 2, LANES), wide(2, LANES), wide(n_rep, 2, LANES),
             dma((12,)),
             dma((2 * n_graph,)), dma((2 * n_graph,)),
-            dma((2 * n_graph,)), dma((2 * n_graph,)), dma((9,)), dma((9,)),
+            dma((2 * n_graph,)), dma((2 * n_graph,)), dma((15,)), dma((15,)),
             dma((n_graph,)), dma((n_graph,)), dma((n_rep,)), dma((n_rep,)),
         ]
         + sum(groups, [])

time: 37.9 us -> 37.6 us (level)
  no operation moved by 1% of the time
where the time goes in v4:
time: 37.6 us; the launch traced here: 37.4 us
  Pallas kernels  36.8 us (98%)
  between operations  0.65 us (2%)
    pallas_call x1, Pallas kernels, on_device(): pl.pallas_call(functools.partial(kernel, n_graph, n_rep), out_shape=(sds(...  35.7 us
    pallas_call x1, Pallas kernels, on_device(): pl.pallas_call(functools.partial(unpack, (n_graph * n_rep * G * B) ** (-0...  1.08 us

profile of v4, /device:TPU:0, one launch (start us, length us, event | category | flops | bytes accessed | tf_op | source)
XLA Modules:
  0.0 37.4 jit_solution(7720829701061071536)
XLA Ops:
  0.6 35.7 %shard_map.179 = (bf16[8,32,256]{2,1,0:T(8,128)(2,1)S(1)}, bf16[8,32,256]{2,1,0:T(8,128)(2,1)S(1)}, bf16[768,128]{1,0:T(8,128)(2,1)S(1)}, bf16[512,128]{1,0:T(8,...) custom-call(s32[1,8]{1,0:T(1,128)} %refs_0_.1, s32[1,8]{1,0:T(1,128)} %refs_1_.1, ...), custom_call_target="tpu_custom_call" | custom-call | tf_op jit(solution)/shard_map/pallas_call | solution.py:682
  36.3 1.1 %shard_map.180 = (bf16[8,32,256]{2,1,0:T(8,128)(2,1)}, bf16[8,32,256]{2,1,0:T(8,128)(2,1)}, f32[128,512]{1,0:T(8,128)}, f32[1,128]{1,0:T(1,128)}, f32[128,256]{1...) custom-call(bf16[8,32,256]{2,1,0:T(8,128)(2,1)S(1)} %get-tuple-element.22.updated, ...), custom_call_target="tpu_custom_call" | custom-call | tf_op jit(solution)/shard_map/pallas_call | solution.py:700
